TPU v7x, 256 devices: a whole 4x4x8 slice. The times are simulated.
256 devices in a mesh: dp: 128 (over y, x_hi, z, core), mp: 2 (over x_lo).
Axes of the slice: x: 4 (x_hi: 2, x_lo: 2; x = x_hi * 2 + x_lo), y: 4, z: 8, core: 2. Of those that a mesh axis runs over, the one named last changes fastest.
Arguments:
- dino_tokens: bfloat16 [65536, 1024], P('dp', 'mp'), may hold values from -6 to 6
- siglip_tokens: bfloat16 [65536, 1152], P('dp', 'mp'), may hold values from -6 to 6
- dino_norm_one: float32 [1024], replicated, may hold values from 0.25 to 1.75
- dino_qkv: bfloat16 [1024, 3, 1024], P('dp', None, 'mp'), may hold values from -6.05625 to 6.05625
- dino_out: bfloat16 [1024, 1024], P('mp', 'dp'), may hold values from -0.1875 to 0.1875
- dino_norm_two: float32 [1024], replicated, may hold values from 0.25 to 1.75
- dino_up: bfloat16 [1024, 4096], P('dp', 'mp'), may hold values from -0.1875 to 0.1875
- dino_down: bfloat16 [4096, 1024], P('mp', 'dp'), may hold values from -0.09375 to 0.09375
- siglip_norm_one: float32 [1152], replicated, may hold values from 0.25 to 1.75
- siglip_qkv: bfloat16 [1152, 3, 1152], P('dp', None, 'mp'), may hold values from -5.709887 to 5.709887
- siglip_out: bfloat16 [1152, 1152], P('mp', 'dp'), may hold values from -0.1875 to 0.1875
- siglip_norm_two: float32 [1152], replicated, may hold values from 0.25 to 1.75
- siglip_up: bfloat16 [1152, 4304], P('dp', 'mp'), may hold values from -0.1875 to 0.1875
- siglip_down: bfloat16 [4304, 1152], P('mp', 'dp'), may hold values from -0.09375 to 0.09375
Outputs:
- dino_result: bfloat16 [65536, 1024], P('dp', 'mp')
- siglip_result: bfloat16 [65536, 1152], P('dp', 'mp')
All inputs are finite; a program needn't handle non-finite values.
Results may differ from a plain program's by a relative error of at most 0.012.
Values may be sent and summed in bfloat16 or wider, within the bound.
A program may use at most 128 MiB of HBM per device.

v0:
```python
import math

import jax
import jax.numpy as jnp
from jax import lax
from jax.sharding import PartitionSpec as P

HEADS = 16
PATCHES = 256


EPS = 1e-06


def from_everyone(shard, axis):
    size = lax.axis_size(axis)
    return lax.all_to_all(
        jnp.broadcast_to(shard[None], (size, *shard.shape)), axis, 0, 0, tiled=True
    )


def laid_out(pieces, dim):
    shape = list(pieces.shape[1:])
    shape[dim] *= pieces.shape[0]
    return jnp.moveaxis(pieces, 0, dim).reshape(shape)


def gathered_copies(shard, axis, dim):
    pieces = from_everyone(shard, axis)
    return laid_out(pieces, dim)


def split_up(shard, dim, size):
    shape = shard.shape
    pieces = shard.reshape(*shape[:dim], size, shape[dim] // size, *shape[dim + 1 :])
    return jnp.moveaxis(pieces, dim, 0)


def sum_at_owner(shard, axis, dim):
    pieces = split_up(shard, dim, lax.axis_size(axis))
    arrived = lax.all_to_all(pieces, axis, split_axis=0, concat_axis=0, tiled=True)
    return arrived.astype(jnp.float32).sum(axis=0)


def layer_norm(values, gain):
    values = values.astype(jnp.float32)
    center = values - jnp.mean(values, axis=-1, keepdims=True)
    spread = jnp.mean(center * center, axis=-1, keepdims=True)
    return (center * lax.rsqrt(spread + EPS) * gain).astype(jnp.bfloat16)


def encoder(tokens, norm_one, qkv_weight, out_weight, norm_two, up_weight, down_weight, approx):
    rows, local_width = tokens.shape
    whole = gathered_copies(tokens, "mp", 1)
    width = whole.shape[1]
    head_size = width // HEADS
    local_heads = qkv_weight.shape[2] // head_size
    scale = 1.0 / math.sqrt(head_size)
    normed = layer_norm(whole, norm_one)

    def fold_rows(source, piece):
        count = piece.shape[0]
        return jnp.dot(source, piece.reshape(count, -1), preferred_element_type=jnp.float32)

    qkv = fold_rows(normed, lax.all_gather(qkv_weight, "dp", axis=0, tiled=True))
    qkv = qkv.astype(jnp.bfloat16).reshape(rows // PATCHES, PATCHES, 3, local_heads, head_size)
    query = qkv[:, :, 0]
    keys = qkv[:, :, 1]
    values = qkv[:, :, 2]
    scores = jnp.einsum("fqhd,fkhd->fhqk", query, keys, preferred_element_type=jnp.float32) * scale
    top = jnp.max(scores, axis=-1, keepdims=True)
    expo = jnp.exp(scores - top)
    probs = (expo / jnp.sum(expo, axis=-1, keepdims=True)).astype(jnp.bfloat16)
    context = jnp.einsum("fhqk,fkhd->fqhd", probs, values, preferred_element_type=jnp.float32)
    context = context.astype(jnp.bfloat16).reshape(rows, local_heads * head_size)
    partial_attn = jnp.dot(
        context,
        lax.all_gather(out_weight, "dp", axis=1, tiled=True),
        preferred_element_type=jnp.float32,
    )
    share = sum_at_owner(partial_attn.astype(jnp.bfloat16), "mp", 1)
    middle = (tokens.astype(jnp.float32) + share).astype(jnp.bfloat16)
    middle_whole = gathered_copies(middle, "mp", 1)
    second = layer_norm(middle_whole, norm_two)
    raised = fold_rows(second, lax.all_gather(up_weight, "dp", axis=0, tiled=True))
    hidden = jax.nn.gelu(raised, approximate=approx).astype(jnp.bfloat16)
    partial_mlp = jnp.dot(
        hidden,
        lax.all_gather(down_weight, "dp", axis=1, tiled=True),
        preferred_element_type=jnp.float32,
    )
    mlp_part = sum_at_owner(partial_mlp.astype(jnp.bfloat16), "mp", 1)
    return (middle.astype(jnp.float32) + mlp_part).astype(jnp.bfloat16)


def local(
    dino_tokens,
    siglip_tokens,
    dino_norm_one,
    dino_qkv,
    dino_out,
    dino_norm_two,
    dino_up,
    dino_down,
    siglip_norm_one,
    siglip_qkv,
    siglip_out,
    siglip_norm_two,
    siglip_up,
    siglip_down,
):
    dino_result = encoder(
        dino_tokens, dino_norm_one, dino_qkv, dino_out, dino_norm_two, dino_up, dino_down, False
    )
    siglip_result = encoder(
        siglip_tokens,
        siglip_norm_one,
        siglip_qkv,
        siglip_out,
        siglip_norm_two,
        siglip_up,
        siglip_down,
        True,
    )
    return (dino_result, siglip_result)


def solution(mesh):
    in_specs = (
        P("dp", "mp"),
        P("dp", "mp"),
        P(),
        P("dp", None, "mp"),
        P("mp", "dp"),
        P(),
        P("dp", "mp"),
        P("mp", "dp"),
        P(),
        P("dp", None, "mp"),
        P("mp", "dp"),
        P(),
        P("dp", "mp"),
        P("mp", "dp"),
    )
    out_specs = (P("dp", "mp"), P("dp", "mp"))
    return jax.shard_map(local, mesh=mesh, in_specs=in_specs, out_specs=out_specs, check_vma=False)
```

profile of v0, /device:TPU:1, one launch (start us, length us, event | category | flops | bytes accessed | tf_op | source)
XLA Modules:
  0.0 1024.8 jit_solution(13799758242859776503)
XLA Ops:
  7.2 0.7 all-gather.12.cloned.1.call-update
  8.0 0.7 all-gather.14.cloned.1.call-update
  8.7 0.7 all-gather.22.cloned.1.call-update
  11.2 0.7 all-gather.24.cloned.1.call-update
  11.9 1.3 copy.43
  13.2 1.1 broadcast_in_dim.8
  14.2 3.6 all-to-all-start
  17.8 11.6 %all-to-all-done = bf16[2,512,512]{1,2,0:T(8,128)(2,1)S(1)} async-done(((bf16[2,512,512]{1,2,0:T(8,128)(2,1)}), bf16[2,512,512]{1,2,0:T(8,128)(2,1)S(1)}, u32[]{:S(2)}, u32[]{:S(2)}) %all-to-all-start) | async-done | bytes 1048608 | tf_op jit(solution)/shard_map/all_to_all | solution.py:17
  29.4 1.1 broadcast_in_dim.10
  30.6 3.6 all-to-all-start.4
  34.7 1.3 fusion.43
  36.1 90.8 %all-gather.12.cloned.1.call-done = bf16[1024,3,512]{2,0,1:T(8,128)(2,1)} async-done(((bf16[8,3,512]{2,0,1:T(8,128)(2,1)}), bf16[1024,3,512]{2,0,1:T(8,128)(2,1)}) %all-gather.12.cloned.1.call-update) | async-done | bytes 3145744 | tf_op jit(solution)/shard_map/all_gather | solution.py:65
  126.8 4.7 copy.44
  131.5 4.1 convolution_convert_fusion.2
  135.6 3.2 reshape.172
  138.7 3.1 fusion.101
  141.8 2.5 copy.67
  144.3 1.4 copy.68
  145.7 0.6 copy.66
  146.3 2.0 fusion.61
  148.3 3.2 fusion.103
  152.7 78.1 %all-gather.14.cloned.1.call-done = bf16[512,1024]{0,1:T(8,128)(2,1)} async-done(((bf16[512,8]{0,1:T(8,128)(2,1)}), bf16[512,1024]{0,1:T(8,128)(2,1)}) %all-gather.14.cloned.1.call-update) | async-done | bytes 1048592 | tf_op jit(solution)/shard_map/all_gather | solution.py:78
  230.8 2.0 convolution_convert_fusion.4
  232.8 1.1 copy.85
  233.9 3.6 all-to-all-start.1
  237.5 0.7 all-gather.26.cloned.1.call-update
  238.5 12.6 %all-to-all-done.1 = bf16[2,512,512]{2,1,0:T(8,128)(2,1)S(1)} async-done(((bf16[2,512,512]{2,1,0:T(8,128)(2,1)}), bf16[2,512,512]{2,1,0:T(8,128)(2,1)S(1)}, u32[]{:S(2)}, u32[]{:S(2)}) %all-to-all-start.1) | async-done | bytes 1048608 | tf_op jit(solution)/shard_map/all_to_all | solution.py:41
  251.7 1.1 broadcast_in_dim.9
  252.8 3.8 all-to-all-start.2
  256.9 1.4 fusion.32
  258.3 91.3 %all-gather.22.cloned.1.call-done = bf16[128,9,576]{2,1,0:T(8,128)(2,1)} async-done(((bf16[1,9,576]{2,1,0:T(8,128)(2,1)}), bf16[128,9,576]{2,1,0:T(8,128)(2,1)}) %all-gather.22.cloned.1.call-update) | async-done | bytes 1327120 | tf_op jit(solution)/shard_map/all_gather | solution.py:78
  349.6 4.1 reshape.167
  353.9 118.7 %all-gather.20.cloned.1.call-done = bf16[1152,3,576]{2,1,0:T(4,128)(2,1)} async-done(((bf16[9,3,576]{2,1,0:T(4,128)(2,1)}), bf16[1152,3,576]{2,1,0:T(4,128)(2,1)}) %all-gather.20.cloned.1.call-update) | async-done | bytes 3981328 | tf_op jit(solution)/shard_map/all_gather | solution.py:65
  472.6 11.3 %copy.54 = bf16[1152,3,576]{0,2,1:T(8,128)(2,1)} copy(bf16[1152,3,576]{2,1,0:T(4,128)(2,1)} %all-gather.20.cloned.1.call-done) | data formatting | bytes 7962624 | tf_op jit(solution)/shard_map/all_gather | solution.py:65
  484.0 5.8 convolution_convert_fusion
  489.8 4.8 reshape.160
  494.6 2.6 fusion.102
  497.2 0.8 fusion.60
  498.0 3.2 fusion.104
  501.7 0.6 copy.59
  502.6 1.3 convolution_convert_fusion.1
  503.9 1.5 copy.60
  505.3 3.7 all-to-all-start.5
  509.4 1.3 fusion.46
  510.7 13.2 %all-to-all-done.5 = bf16[2,512,576]{1,2,0:T(8,128)(2,1)S(1)} async-done(((bf16[2,512,576]{1,2,0:T(8,128)(2,1)}), bf16[2,512,576]{1,2,0:T(8,128)(2,1)S(1)}, u32[]{:S(2)}, u32[]{:S(2)}) %all-to-all-start.5) | async-done | bytes 1179680 | tf_op jit(solution)/shard_map/all_to_all | solution.py:41
  524.4 1.1 broadcast_in_dim.11
  525.5 3.8 all-to-all-start.6
  529.3 63.4 %all-gather.16.cloned.1.call-done = bf16[1024,2048]{1,0:T(8,128)(2,1)} async-done(((bf16[8,2048]{1,0:T(8,128)(2,1)}), bf16[1024,2048]{1,0:T(8,128)(2,1)}) %all-gather.16.cloned.1.call-update) | async-done | bytes 4194320 | tf_op jit(solution)/shard_map/all_gather | solution.py:85
  592.7 120.0 %all-gather.18.cloned.1.call-done = bf16[2048,1024]{0,1:T(8,128)(2,1)} async-done(((bf16[2048,8]{0,1:T(8,128)(2,1)}), bf16[2048,1024]{0,1:T(8,128)(2,1)}) %all-gather.18.cloned.1.call-update) | async-done | bytes 4194320 | tf_op jit(solution)/shard_map/all_gather | solution.py:89
  712.7 18.0 %fusion.53 = bf16[512,1024]{1,0:T(8,128)(2,1)} fusion(bf16[2048,1024]{0,1:T(8,128)(2,1)} %all-gather.18.cloned.1.call-done, bf16[512,1024]{0,1:T(8,128)(2,1)} %fusion.46, bf16[1024,2048]{1,0:T(8,128)(2,1)} %all-gather.16.cloned.1.call-done), kind=kOutput, calls=%fused_computation.79 | convolution fusion | flops 4363649024 | bytes 10485760 | tf_op jit(solution)/shard_map/dot_general | solution.py:87
  730.7 2.3 copy.84
  733.0 4.5 all-to-all-start.3
  738.1 1.4 fusion.35
  739.5 103.9 %all-gather.24.cloned.1.call-done = bf16[128,9,2152]{2,1,0:T(8,128)(2,1)} async-done(((bf16[1,9,2152]{2,1,0:T(8,128)(2,1)}), bf16[128,9,2152]{2,1,0:T(8,128)(2,1)}) %all-gather.24.cloned.1.call-update) | async-done | bytes 4958224 | tf_op jit(solution)/shard_map/all_gather | solution.py:85
  843.4 9.1 reshape.169
  852.5 121.5 %all-gather.26.cloned.1.call-done = bf16[128,9,2152]{2,1,0:T(8,128)(2,1)} async-done(((bf16[1,9,2152]{2,1,0:T(8,128)(2,1)}), bf16[128,9,2152]{2,1,0:T(8,128)(2,1)}) %all-gather.26.cloned.1.call-update) | async-done | bytes 4958224 | tf_op jit(solution)/shard_map/all_gather | solution.py:89
  974.1 9.1 reshape.171
  983.2 12.2 %convolution_convert_fusion.3 = bf16[512,1152]{1,0:T(8,128)(2,1)} fusion(bf16[1152,2152]{1,0:T(8,128)(2,1)} %reshape.171, bf16[512,1152]{0,1:T(8,128)(2,1)S(1)} %copy-done.5, bf16[1152,2152]{1,0:T(8,128)(2,1)} %reshape.169), kind=kOutput, calls=%fused_computation.41 | convolution fusion | flops 5087711232 | bytes 12275712 | tf_op jit(solution)/shard_map/dot_general | solution.py:87
  995.4 2.4 copy.61
  997.8 3.6 all-to-all-start.7
  1001.4 1.5 convert_reduce_fusion.4
  1002.9 1.0 add_convert_fusion.2
  1003.9 12.4 %all-to-all-done.7 = bf16[2,512,576]{1,2,0:T(8,128)(2,1)S(1)} async-done(((bf16[2,512,576]{1,2,0:T(8,128)(2,1)}), bf16[2,512,576]{1,2,0:T(8,128)(2,1)S(1)}, u32[]{:S(2)}, u32[]{:S(2)}) %all-to-all-start.7) | async-done | bytes 1179680 | tf_op jit(solution)/shard_map/all_to_all | solution.py:41
  1016.5 1.0 add_convert_fusion
  (64 shorter events, 7.4 us)
Async XLA Ops:
  7.2 10.7 %copy-start.9 = (f32[1024]{0:T(1024)S(1)}, f32[1024]{0:T(1024)}, u32[]{:S(2)}) copy-start(f32[1024]{0:T(1024)} %param.16) | copy-start | bytes 12292
  7.2 22.3 %copy-start = (bf16[512,576]{0,1:T(8,128)(2,1)S(1)}, bf16[512,576]{0,1:T(8,128)(2,1)}, u32[]{:S(2)}) copy-start(bf16[512,576]{0,1:T(8,128)(2,1)} %param.15) | copy-start | bytes 1769476
  7.2 119.6 %all-gather.12.cloned.1.call-start = ((), (), s32[]{:S(2)}) async-start(), calls=%async_computation.8 | async-start | bytes 3170304 | tf_op jit(solution)/shard_map/all_gather | solution.py:65
  7.9 222.9 %all-gather.14.cloned.1.call-start = ((), (), s32[]{:S(2)}) async-start(), calls=%async_computation.9 | async-start | bytes 1056768 | tf_op jit(solution)/shard_map/all_gather | solution.py:78
  8.7 340.9 %all-gather.22.cloned.1.call-start = ((), (), s32[]{:S(2)}) async-start(), calls=%async_computation.13 | async-start | bytes 2641920 | tf_op jit(solution)/shard_map/all_gather | solution.py:78
  9.4 463.2 %all-gather.20.cloned.1.call-start = ((), (), s32[]{:S(2)}) async-start(), calls=%async_computation.12 | async-start | bytes 5944320 | tf_op jit(solution)/shard_map/all_gather | solution.py:65
  10.0 582.7 %all-gather.16.cloned.1.call-start = ((), (), s32[]{:S(2)}) async-start(), calls=%async_computation.10 | async-start | bytes 4227072 | tf_op jit(solution)/shard_map/all_gather | solution.py:85
  10.6 702.2 %all-gather.18.cloned.1.call-start = ((), (), s32[]{:S(2)}) async-start(), calls=%async_computation.11 | async-start | bytes 4227072 | tf_op jit(solution)/shard_map/all_gather | solution.py:89
  11.1 832.3 %all-gather.24.cloned.1.call-start = ((), (), s32[]{:S(2)}) async-start(), calls=%async_computation.14 | async-start | bytes 8982528 | tf_op jit(solution)/shard_map/all_gather | solution.py:85
  14.2 15.2 %all-to-all-start = ((bf16[2,512,512]{1,2,0:T(8,128)(2,1)}), bf16[2,512,512]{1,2,0:T(8,128)(2,1)S(1)}, u32[]{:S(2)}, u32[]{:S(2)}) async-start(bf16[2,512,512]{1,2,0:T(8,128)(2,1)} %broadcast_in_dim.8), calls=%async_computation | async-start | bytes 2097152 | tf_op jit(solution)/shard_map/all_to_all | solution.py:17
  30.6 203.3 %all-to-all-start.4 = ((bf16[2,512,576]{1,2,0:T(8,128)(2,1)}), bf16[2,512,576]{1,2,0:T(8,128)(2,1)S(1)}, u32[]{:S(2)}, u32[]{:S(2)}) async-start(bf16[2,512,576]{1,2,0:T(8,128)(2,1)} %broadcast_in_dim.10), calls=%async_computation.4 | async-start | bytes 2359296 | tf_op jit(solution)/shard_map/all_to_all | solution.py:17
  152.6 85.7 %copy-start.7 = (f32[1152]{0:T(1024)S(1)}, f32[1152]{0:T(1024)}, u32[]{:S(2)}) copy-start(f32[1152]{0:T(1024)} %param.22) | copy-start | bytes 13828
  232.8 18.5 %copy-start.2 = (bf16[512,512]{1,0:T(8,128)(2,1)S(1)}, bf16[512,512]{1,0:T(8,128)(2,1)}, u32[]{:S(2)}) copy-start(bf16[512,512]{1,0:T(8,128)(2,1)} %param.14) | copy-start | bytes 1572868
  233.9 17.2 %all-to-all-start.1 = ((bf16[2,512,512]{2,1,0:T(8,128)(2,1)}), bf16[2,512,512]{2,1,0:T(8,128)(2,1)S(1)}, u32[]{:S(2)}, u32[]{:S(2)}) async-start(bf16[2,512,512]{2,1,0:T(8,128)(2,1)} %bitcast.102), calls=%async_computation.1 | async-start | bytes 2097152 | tf_op jit(solution)/shard_map/all_to_all | solution.py:41
  237.5 736.6 %all-gather.26.cloned.1.call-start = ((), (), s32[]{:S(2)}) async-start(), calls=%async_computation.15 | async-start | bytes 8982528 | tf_op jit(solution)/shard_map/all_gather | solution.py:89
  252.8 100.9 %all-to-all-start.2 = ((bf16[2,512,512]{1,2,0:T(8,128)(2,1)}), bf16[2,512,512]{1,2,0:T(8,128)(2,1)S(1)}, u32[]{:S(2)}, u32[]{:S(2)}) async-start(bf16[2,512,512]{1,2,0:T(8,128)(2,1)} %broadcast_in_dim.9), calls=%async_computation.2 | async-start | bytes 2097152 | tf_op jit(solution)/shard_map/all_to_all | solution.py:17
  353.9 130.0 %copy-start.4 = (bf16[2,512,576]{1,2,0:T(8,128)(2,1)S(1)}, bf16[2,512,576]{1,2,0:T(8,128)(2,1)}, u32[]{:S(2)}) copy-start(bf16[2,512,576]{1,2,0:T(8,128)(2,1)} %fusion.32) | copy-start | bytes 3538948
  501.2 1.4 copy-start.3
  502.6 6.8 copy-start.8
  505.3 18.8 %copy-start.1 = (bf16[512,576]{0,1:T(8,128)(2,1)S(1)}, bf16[512,576]{0,1:T(8,128)(2,1)}, u32[]{:S(2)}) copy-start(bf16[512,576]{0,1:T(8,128)(2,1)} %param.15) | copy-start | bytes 1769476
  505.3 18.6 %all-to-all-start.5 = ((bf16[2,512,576]{1,2,0:T(8,128)(2,1)}), bf16[2,512,576]{1,2,0:T(8,128)(2,1)S(1)}, u32[]{:S(2)}, u32[]{:S(2)}) async-start(bf16[2,512,576]{1,2,0:T(8,128)(2,1)} %bitcast.21), calls=%async_computation.5 | async-start | bytes 2359296 | tf_op jit(solution)/shard_map/all_to_all | solution.py:41
  525.5 207.5 %all-to-all-start.6 = ((bf16[2,512,576]{1,2,0:T(8,128)(2,1)}), bf16[2,512,576]{1,2,0:T(8,128)(2,1)S(1)}, u32[]{:S(2)}, u32[]{:S(2)}) async-start(bf16[2,512,576]{1,2,0:T(8,128)(2,1)} %broadcast_in_dim.11), calls=%async_computation.6 | async-start | bytes 2359296 | tf_op jit(solution)/shard_map/all_to_all | solution.py:17
  730.7 7.4 copy-start.6
  733.0 264.8 %all-to-all-start.3 = ((bf16[2,512,512]{2,1,0:T(8,128)(2,1)}), bf16[2,512,512]{2,1,0:T(8,128)(2,1)}, u32[]{:S(2)}, u32[]{:S(2)}) async-start(bf16[2,512,512]{2,1,0:T(8,128)(2,1)} %bitcast.103), calls=%async_computation.3 | async-start | bytes 2097152 | tf_op jit(solution)/shard_map/all_to_all | solution.py:41
  852.5 130.7 %copy-start.5 = (bf16[512,1152]{0,1:T(8,128)(2,1)S(1)}, bf16[512,1152]{0,1:T(8,128)(2,1)}, u32[]{:S(2)}) copy-start(bf16[512,1152]{0,1:T(8,128)(2,1)} %fusion.35) | copy-start | bytes 3538948
  997.8 18.4 %all-to-all-start.7 = ((bf16[2,512,576]{1,2,0:T(8,128)(2,1)}), bf16[2,512,576]{1,2,0:T(8,128)(2,1)S(1)}, u32[]{:S(2)}, u32[]{:S(2)}) async-start(bf16[2,512,576]{1,2,0:T(8,128)(2,1)} %bitcast.28), calls=%async_computation.7 | async-start | bytes 2359296 | tf_op jit(solution)/shard_map/all_to_all | solution.py:41
Sparse Core Ops, SparseCore 0:
  11.8 114.9 all-gather.11
  130.6 100.1 all-gather.13
  234.4 115.1 all-gather.21
  353.1 119.4 all-gather.19
  476.1 116.5 all-gather.15
  596.1 116.5 all-gather.17
  716.3 127.0 all-gather.23
  847.0 127.0 all-gather.25
where the time goes:
time: 1030 us; the launch traced here: 1020 us
  waiting for transfers between devices  842 us (82%)
  local copies, waits for them, and re-layouts  71.3 us (7%)
  matrix products  46.9 us (5%)
  starting transfers between devices  30.4 us (3%)
  other arithmetic  18.8 us (2%)
  between operations  14.9 us (1%)
    all_gather x2, waiting for transfers between devices, encoder(): lax.all_gather(down_weight, 'dp', axis=1, tiled=True)  242 us
    all_gather x2, waiting for transfers between devices, encoder(): lax.all_gather(qkv_weight, 'dp', axis=0, tiled=True)  209 us
    all_gather x2, waiting for transfers between devices, encoder(): lax.all_gather(out_weight, 'dp', axis=1, tiled=True)  169 us
    all_gather x2, waiting for transfers between devices, encoder(): lax.all_gather(up_weight, 'dp', axis=0, tiled=True)  167 us
    all_to_all x4, waiting for transfers between devices, sum_at_owner(): lax.all_to_all(pieces, axis, split_axis=0, concat_axis=0, tiled=True)  38.1 us
    dot_general x2, matrix products, encoder(): jnp.dot(hidden, lax.all_gather(down_weight, 'dp', axis=1, tiled=True), pr...  30.2 us
    unnamed x29, local copies, waits for them, and re-layouts  28.5 us
  transfers between devices with their start and end apart: 16, of which 12 were waited for; matrix products, arithmetic and copies ran while one was open for 13% of the time, Pallas kernels for 0%

commit v1 on v0

v1 whole, which is shorter than its diff:
```python
import functools
import heapq
import math

import jax
import jax.numpy as jnp
from jax import lax
from jax.experimental import pallas as pl
from jax.experimental.pallas import tpu as pltpu
from jax.sharding import PartitionSpec as P

HEADS = 16
LOCAL = HEADS // 2
PATCHES = 256
EPS = 1e-06
BF = jnp.bfloat16
F32 = jnp.float32

Y, XH, Z, C = 4, 2, 8, 2


RING = {"y": Y, "z": Z}


def onward(order, piece):
    dy, dz, dx, half = piece
    place = {"y": dy, "z": dz}

    def ring(axis):
        d, n = place[axis], RING[axis]

        def at(to, h):
            spot = dict(place, **{axis: to})
            return (spot["y"], spot["z"], dx, h)

        if d == 0:
            return [(axis + "+", at(-1, half)), (axis + "-", at(1, half))]
        if d < 0 and -d < n // 2 - 1:
            return [(axis + "+", at(d - 1, half))]
        if d > 0 and d < n // 2 - 1:
            return [(axis + "-", at(d + 1, half))]
        if d == 1 - n // 2 and half != 1:
            return [(axis + "+", at(-n // 2, 0))]
        if d == n // 2 - 1 and half != 0:
            return [(axis + "-", at(-n // 2, 1))]
        return []

    first, second = order
    sends = ring(first) if place[second] == 0 else []
    return sends + ring(second)


def arrivals(streams, rate=0.044, hop=2.0, across=9.0):
    free = dict.fromkeys(("y+", "y-", "z+", "z-"), 0.0)
    events, order = [], []
    for s in range(len(streams)):
        events += [(0.0, len(events), s, (0, 0, 0, None)), (across, len(events) + 1, s, (0, 0, 1, None))]
    heapq.heapify(events)
    count = len(events)
    while events:
        t, _, s, piece = heapq.heappop(events)
        order.append((s, piece))
        for link, child in onward(streams[s][0], piece):
            size = streams[s][2] * (1.0 if child[3] is None else 0.5)
            free[link] = max(free[link], t) + size * rate
            count += 1
            heapq.heappush(events, (free[link] + hop, count, s, child))
    return order


def gather_kernel(streams, order, block, dino, siglip, w, dino_got, siglip_got, send, recv, pass_send, pass_recv, more_send, more_recv, near):
    me, mp = lax.axis_index("dp"), lax.axis_index("mp")
    c, z, xh, y = lax.rem(me, 2), lax.rem(me // 2, 8), lax.rem(me // 16, 2), me // 32

    def at(y, xh, z, c):
        return ((y * XH + xh) * Z + z) * C + c

    up_y, down_y = lax.rem(y + 1, Y), lax.rem(y + Y - 1, Y)
    up_z, down_z = lax.rem(z + 1, Z), lax.rem(z + Z - 1, Z)
    to = {
        "y+": (at(up_y, xh, z, c), mp),
        "y-": (at(down_y, xh, z, c), mp),
        "z+": (at(y, xh, up_z, c), mp),
        "z-": (at(y, xh, down_z, c), mp),
        "x": (at(y, 1 - xh, z, c), mp),
        "core": (at(y, xh, z, 1 - c), mp),
        "mp": (me, 1 - mp),
    }
    number = {event: i for i, event in enumerate(order)}

    def columns(s, half):
        _, start, tiles = streams[s]
        low, high = {None: (0, tiles), 0: (0, tiles // 2), 1: (tiles // 2, tiles)}[half]
        return slice((start + low) * 128, (start + high) * 128)

    def spot(s, piece, half=None):
        dy, dz, dx, mine = piece
        half = mine if half is None else half
        source = (lax.rem(y + dy + Y, Y), lax.rem(z + dz + Z, Z), c, lax.rem(xh + dx, 2))
        return w.at[(*source, slice(None), columns(s, half))]

    def remote(src, dst, sends, receives, k, link):
        return pltpu.make_async_remote_copy(
            src_ref=src,
            dst_ref=dst,
            send_sem=sends.at[k],
            recv_sem=receives.at[k],
            device_id=to[link],
            device_id_type=pl.DeviceIdType.MESH,
        )

    def source_of(s, piece, half):
        if piece[:3] == (0, 0, 0):
            return block.at[:, columns(s, half)]
        return spot(s, piece, half)

    def hop(s, piece, link, child):
        return remote(source_of(s, piece, child[3]), spot(s, piece, child[3]), send, recv, number[(s, child)], link)

    def share(s, piece):
        k = number[(s, piece)]
        return remote(source_of(s, piece, piece[3]), spot(s, piece), pass_send, pass_recv, k, "core")

    def arrived(s, piece):
        k = number[(s, piece)]
        return remote(spot(s, piece), spot(s, piece), send, recv, k, "y+")

    barrier = pltpu.get_barrier_semaphore()
    for device in to.values():
        pl.semaphore_signal(barrier, inc=1, device_id=device, device_id_type=pl.DeviceIdType.MESH)
    pl.semaphore_wait(barrier, len(to))

    own = [s for s in range(len(streams))]
    across = [hop(s, (0, 0, 0, None), "x", (0, 0, 1, None)) for s in own]
    tokens = [
        remote(dino, dino_got, more_send, more_recv, 0, "mp"),
        remote(siglip, siglip_got, more_send, more_recv, 1, "mp"),
    ]
    for copy in across:
        copy.start()
    started = []
    for i, (s, piece) in enumerate(order):
        if piece != (0, 0, 0, None):
            arrived(s, piece).wait_recv()
        for link, child in onward(streams[s][0], piece):
            copy = hop(s, piece, link, child)
            copy.start()
            started.append(copy)
        copy = share(s, piece)
        copy.start()
        if i == len(streams) - 1:
            for copy in tokens:
                copy.start()
            mine = pltpu.make_async_copy(block, w.at[y, z, c, xh], near)
            mine.start()
    for copy in started + across:
        copy.wait_send()
    for s, piece in order:
        copy = share(s, piece)
        copy.wait_send()
        dy, dz, dx, half = piece
        source = (lax.rem(y + dy + Y, Y), lax.rem(z + dz + Z, Z), 1 - c, lax.rem(xh + dx, 2))
        there = w.at[(*source, slice(None), columns(s, half))]
        remote(there, there, pass_send, pass_recv, number[(s, piece)], "core").wait_recv()
    for copy in tokens:
        copy.wait()
    mine.wait()


def gather(block, dino, siglip, split):
    tiles = block.shape[1] // 128
    streams = (("yz", 0, split), ("zy", split, tiles - split))
    order = arrivals(streams)
    hbm = pl.BlockSpec(memory_space=pl.ANY)
    dma = pltpu.SemaphoreType.DMA
    n = len(order)
    w, dino_got, siglip_got = pl.pallas_call(
        functools.partial(gather_kernel, streams, order),
        out_shape=(
            jax.ShapeDtypeStruct((Y, Z, C, XH, *block.shape), BF),
            jax.ShapeDtypeStruct(dino.shape, BF),
            jax.ShapeDtypeStruct(siglip.shape, BF),
        ),
        in_specs=[pl.BlockSpec(memory_space=pltpu.VMEM), hbm, hbm],
        out_specs=(hbm, hbm, hbm),
        scratch_shapes=[dma((n,)), dma((n,)), dma((n,)), dma((n,)), dma((2,)), dma((2,)), dma],
        compiler_params=pltpu.CompilerParams(
            collective_id=0, has_side_effects=True, vmem_limit_bytes=16 << 20
        ),
        cost_estimate=pl.CostEstimate(flops=1 << 30, bytes_accessed=32 << 20, transcendentals=0),
        name="gather",
    )(block, dino, siglip)
    return w.reshape(1024, block.shape[1]), dino_got, siglip_got


def widen(x, to):
    return jnp.pad(x, ((0, 0), (0, to - x.shape[1])))


def extra_block(rows, widths, columns):
    flat = jnp.concatenate([widen(r, w).reshape(-1) for r, w in zip(rows, widths)])
    return jnp.pad(flat, (0, 8 * columns - flat.shape[0])).reshape(8, columns)


def one_hot(per_device):
    width = 64 * per_device
    held = lax.broadcasted_iota(jnp.int32, (width, width), 1)
    slot = jnp.where(held < 512, held // 8, held - 512)
    row = jnp.where(held < 512, held % 8, 8)
    xh, c, z, y = slot % 2, (slot // 2) % 2, (slot // 4) % 8, slot // 32
    natural = (((y * XH + xh) * Z + z) * C + c) * per_device + row
    return (lax.broadcasted_iota(jnp.int32, (width, width), 0) == natural).astype(BF)


def held_gain(gain, per_device):
    parts = gain.reshape(Y, XH, Z, C, per_device).transpose(0, 2, 3, 1, 4).reshape(128, per_device)
    held = parts[:, :8].reshape(-1)
    if per_device == 9:
        held = jnp.concatenate([held, parts[:, 8]])
    return held.reshape(1, -1)


def both_halves(mine, other, low):
    a = jnp.where(low, mine, other)
    b = jnp.where(low, other, mine)
    return jnp.concatenate([a[:, :512], b[:, :512], a[:, 512:], b[:, 512:]], axis=1)


def half_of(whole, first):
    low = jnp.concatenate([whole[:, :512], whole[:, 1024 : 1024 + (whole.shape[1] - 1024) // 2]], axis=1)
    high = jnp.concatenate([whole[:, 512:1024], whole[:, 1024 + (whole.shape[1] - 1024) // 2 :]], axis=1)
    return jnp.where(first, low, high)


def swap(x):
    return lax.ppermute(x, "mp", [(0, 1), (1, 0)])


def normed(x, gain):
    center = x - jnp.mean(x, axis=-1, keepdims=True)
    spread = jnp.mean(center * center, axis=-1, keepdims=True)
    return (center * lax.rsqrt(spread + EPS) * gain).astype(BF)


def dot(a, b):
    return jnp.dot(a, b, preferred_element_type=F32)


def dot_t(a, b):
    return lax.dot_general(a, b, (((1,), (1,)), ((), ())), preferred_element_type=F32)


def gelu(x, approx):
    if approx:
        return jax.nn.gelu(x, approximate=True)
    half = 0.5 * x
    return half + half * lax.erf(x * math.sqrt(0.5))


def attention_kernel(size, at_qkv, n_qkv, at_out, n_out, extra, *refs):
    if extra:
        x_ref, g_ref, w_ref, eq_ref, eo_ref, o_ref, wq, wo, sems = refs
    else:
        x_ref, g_ref, w_ref, o_ref, wq, wo, sems = refs
    first = pltpu.make_async_copy(w_ref.at[:, at_qkv : at_qkv + n_qkv], wq, sems.at[0])
    second = pltpu.make_async_copy(w_ref.at[:, at_out : at_out + n_out], wo, sems.at[1])
    first.start()
    second.start()
    first.wait()
    second.wait()
    scale = 1.0 / math.sqrt(size)
    mine = LOCAL * size

    def frame(f, carry):
        rows = pl.ds(pl.multiple_of(f * PATCHES, PATCHES), PATCHES)
        x = normed(x_ref[rows, :].astype(F32), g_ref[...])
        qkv = dot(x[:, :1024], wq[...])
        if extra:
            qkv = qkv + dot(x[:, 1024:], eq_ref[...])
        qkv = qkv.astype(BF)
        heads = []
        for h in range(LOCAL):
            q, k, v = (qkv[:, j * mine + h * size : j * mine + (h + 1) * size] for j in range(3))
            s = dot_t(q, k)
            e = jnp.exp((s - jnp.max(s, axis=-1, keepdims=True)) * scale)
            total = jnp.sum(e, axis=-1, keepdims=True)
            heads.append((dot(e.astype(BF), v) / total).astype(BF))
        if n_out > mine:
            heads.append(jnp.zeros((PATCHES, n_out - mine), BF))
        ctx = jnp.concatenate(heads, axis=1)
        o_ref[rows, :1024] = dot_t(ctx, wo[...]).astype(BF)
        if extra:
            o_ref[rows, 1024:] = dot_t(ctx, eo_ref[...]).astype(BF)
        return carry

    lax.fori_loop(0, 2, frame, 0)


def attention(x, gain, w, extras, size, at_qkv, n_qkv, at_out, n_out):
    vmem = pl.BlockSpec(memory_space=pltpu.VMEM)
    flops = 2 * x.shape[0] * x.shape[1] * (n_qkv + n_out) + 4 * 2 * LOCAL * PATCHES * PATCHES * size
    return pl.pallas_call(
        functools.partial(attention_kernel, size, at_qkv, n_qkv, at_out, n_out, bool(extras)),
        out_shape=jax.ShapeDtypeStruct(x.shape, BF),
        in_specs=[vmem, vmem, pl.BlockSpec(memory_space=pl.ANY)] + [vmem] * len(extras),
        out_specs=vmem,
        scratch_shapes=[
            pltpu.VMEM((1024, n_qkv), BF),
            pltpu.VMEM((1024, n_out), BF),
            pltpu.SemaphoreType.DMA((2,)),
        ],
        compiler_params=pltpu.CompilerParams(vmem_limit_bytes=48 << 20),
        cost_estimate=pl.CostEstimate(flops=flops, bytes_accessed=8 << 20, transcendentals=1 << 20),
        name="attention",
    )(x, gain, w, *extras)


def mlp_kernel(steps, approx, extra, *refs):
    if extra:
        low_ref, x_ref, p_ref, r_ref, g_ref, u_ref, d_ref, ue_ref, de_ref, keep_ref, send_ref, mid, second, acc = refs
    else:
        low_ref, x_ref, p_ref, r_ref, g_ref, u_ref, d_ref, keep_ref, send_ref, mid, second, acc = refs
    j = pl.program_id(0)

    @pl.when(j == 0)
    def _():
        def rows_of(i, carry):
            rows = pl.ds(pl.multiple_of(i * 128, 128), 128)
            m = x_ref[rows, :].astype(F32) + (p_ref[rows, :].astype(F32) + r_ref[rows, :].astype(F32))
            m = m.astype(BF)
            mid[rows, :] = m
            second[rows, :] = normed(m.astype(F32), g_ref[...])
            return carry

        lax.fori_loop(0, 4, rows_of, 0)

    def rows_of(i, carry):
        rows = pl.ds(pl.multiple_of(i * 256, 256), 256)
        raised = dot(second[rows, :1024], u_ref[...])
        if extra:
            raised = raised + dot(second[rows, 1024:], ue_ref[...])
        hidden = gelu(raised, approx).astype(BF)
        main = dot_t(hidden, d_ref[...])
        rest = dot_t(hidden, de_ref[...]) if extra else None

        @pl.when(j == 0)
        def _():
            acc[rows, :1024] = main
            if extra:
                acc[rows, 1024:] = rest

        @pl.when(j > 0)
        def _():
            acc[rows, :1024] += main
            if extra:
                acc[rows, 1024:] += rest

        return carry

    lax.fori_loop(0, 2, rows_of, 0)

    @pl.when(j == steps - 1)
    def _():
        low = low_ref[0] == 0

        def rows_of(i, carry):
            rows = pl.ds(pl.multiple_of(i * 128, 128), 128)
            part = acc[rows, :]
            m = mid[rows, :].astype(F32)

            def put(keep_at, send_at):
                keep_ref[rows, :512] = m[:, keep_at : keep_at + 512] + part[:, keep_at : keep_at + 512]
                send_ref[rows, :512] = part[:, send_at : send_at + 512].astype(BF)
                if extra:
                    ka, sa = 1024 + keep_at // 8, 1024 + send_at // 8
                    keep_ref[rows, 512:] = m[:, ka : ka + 64] + part[:, ka : ka + 64]
                    send_ref[rows, 512:] = part[:, sa : sa + 64].astype(BF)

            @pl.when(low)
            def _():
                put(0, 512)

            @pl.when(jnp.logical_not(low))
            def _():
                put(512, 0)

            return carry

        lax.fori_loop(0, 4, rows_of, 0)


def mlp(mp, x, part, arrived, gain, w, extras, approx, chunk, steps, at):
    rows, width = x.shape
    half = width // 2
    whole = lambda shape: pl.BlockSpec(shape, lambda j, s: (0, 0))
    in_specs = [whole((rows, width))] * 3 + [whole((1, width))]
    in_specs += [
        pl.BlockSpec((1024, chunk), lambda j, s: (0, at // chunk + j)),
        pl.BlockSpec((1024, chunk), lambda j, s: (0, at // chunk + steps + j)),
    ]
    in_specs += [pl.BlockSpec((128, chunk), lambda j, s: (0, j))] * len(extras)
    flops = 4 * rows * width * chunk * steps
    return pl.pallas_call(
        functools.partial(mlp_kernel, steps, approx, bool(extras)),
        out_shape=(jax.ShapeDtypeStruct((rows, half), F32), jax.ShapeDtypeStruct((rows, half), BF)),
        grid_spec=pltpu.PrefetchScalarGridSpec(
            num_scalar_prefetch=1,
            grid=(steps,),
            in_specs=in_specs,
            out_specs=(whole((rows, half)), whole((rows, half))),
            scratch_shapes=[
                pltpu.VMEM((rows, width), BF),
                pltpu.VMEM((rows, width), BF),
                pltpu.VMEM((rows, width), F32),
            ],
        ),
        compiler_params=pltpu.CompilerParams(
            dimension_semantics=("arbitrary",), vmem_limit_bytes=56 << 20
        ),
        cost_estimate=pl.CostEstimate(flops=flops, bytes_accessed=12 << 20, transcendentals=1 << 20),
        name="mlp",
    )(mp, x, part, arrived, gain, w, w, *extras)


def local(
    dino_tokens,
    siglip_tokens,
    dino_norm_one,
    dino_qkv,
    dino_out,
    dino_norm_two,
    dino_up,
    dino_down,
    siglip_norm_one,
    siglip_qkv,
    siglip_out,
    siglip_norm_two,
    siglip_up,
    siglip_down,
):
    mp = lax.axis_index("mp")
    low = mp == 0
    mp_word = mp.reshape(1).astype(jnp.int32)

    d_out_t, d_down_t = dino_out.T, dino_down.T
    s_qkv = siglip_qkv.reshape(9, -1)
    s_out_t, s_down_t = siglip_out.T, siglip_down.T
    block_one = jnp.concatenate(
        [
            dino_qkv.reshape(8, -1),
            d_out_t,
            widen(s_qkv[:8], 1792),
            widen(s_out_t[:8], 640),
            extra_block([s_qkv[8:], s_out_t[8:]], [1792, 640], 384),
        ],
        axis=1,
    )
    block_two = jnp.concatenate(
        [
            widen(siglip_up[:8], 2304),
            widen(s_down_t[:8], 2304),
            dino_up,
            d_down_t,
            extra_block([siglip_up[8:], s_down_t[8:]], [2304, 2304], 640),
        ],
        axis=1,
    )
    d_hot, s_hot = one_hot(8), one_hot(9)
    d_mine = dot(dino_tokens, d_hot).astype(BF)
    s_mine = dot(siglip_tokens, s_hot).astype(BF)
    w, d_other, s_other = gather(jnp.concatenate([block_two, block_one], axis=1), d_mine, s_mine, 44)
    d_whole = both_halves(d_mine, d_other, low)
    s_whole = both_halves(s_mine, s_other, low)

    s_extra = w[:, 13824:14208].reshape(128, 3072)
    d_part = attention(d_whole, held_gain(dino_norm_one, 8), w, (), 64, 9344, 1536, 10880, 512)
    d_arrived = swap(d_part)
    s_part = attention(
        s_whole, held_gain(siglip_norm_one, 9), w, (s_extra[:, :1792], s_extra[:, 1792:2432]), 72, 11392, 1792, 13184, 640
    )
    s_arrived = swap(s_part)

    s_extra_two = w[:, 8704:9344].reshape(128, 5120)
    d_keep, d_send = mlp(mp_word, d_whole, d_part, d_arrived, held_gain(dino_norm_two, 8), w, (), False, 512, 4, 4608)
    d_got = swap(d_send)
    s_keep, s_send = mlp(
        mp_word,
        s_whole,
        s_part,
        s_arrived,
        held_gain(siglip_norm_two, 9),
        w,
        (s_extra_two[:, :2304], s_extra_two[:, 2304:4608]),
        True,
        768,
        3,
        0,
    )
    s_got = swap(s_send)
    dino_result = dot_t((d_keep + d_got.astype(F32)).astype(BF), d_hot).astype(BF)
    siglip_result = dot_t((s_keep + s_got.astype(F32)).astype(BF), s_hot).astype(BF)
    return (dino_result, siglip_result)


def solution(mesh):
    in_specs = (
        P("dp", "mp"),
        P("dp", "mp"),
        P(),
        P("dp", None, "mp"),
        P("mp", "dp"),
        P(),
        P("dp", "mp"),
        P("mp", "dp"),
        P(),
        P("dp", None, "mp"),
        P("mp", "dp"),
        P(),
        P("dp", "mp"),
        P("mp", "dp"),
    )
    out_specs = (P("dp", "mp"), P("dp", "mp"))
    return jax.shard_map(local, mesh=mesh, in_specs=in_specs, out_specs=out_specs, check_vma=False)
```

time: 1030 us -> 215 us (0.21)
  waiting for transfers between devices: 842 us -> 19 us
  Pallas kernels: 0 us -> 149 us
  matrix products: 46.9 us -> 5.77 us
  local copies, waits for them, and re-layouts: 71.3 us -> 33.7 us
  starting transfers between devices: 30.4 us -> 3.12 us
  other arithmetic: 18.8 us -> 0.44 us
  between operations: 14.9 us -> 1.6 us
    all_gather x8 -> x0, waiting for transfers between devices: 788 us -> none  [the longest x2 242 us: encoder(): lax.all_gather(down_weight, 'dp', axis=1, tiled=True)]
    pallas_call x0 -> x5, Pallas kernels: none -> 149 us  [the longest x1 98.3 us: gather(): pl.pallas_call(functools.partial(gather_kernel, streams, order), out_shap...]
    all_to_all x8 -> x0, waiting for transfers between devices: 49.7 us -> none  [the longest x4 38.1 us: sum_at_owner(): lax.all_to_all(pieces, axis, split_axis=0, concat_axis=0, tiled=True)]
    dot_general x10 -> x4, matrix products: 46.9 us -> 5.77 us  [the longest x2 4.46 us: dot_t(): lax.dot_general(a, b, (((1,), (1,)), ((), ())), preferred_element_type=F32)]
    all_to_all x8 -> x0, starting transfers between devices: 30.1 us -> none  [the longest x4 15.4 us: sum_at_owner(): lax.all_to_all(pieces, axis, split_axis=0, concat_axis=0, tiled=True)]
    ppermute x0 -> x4, waiting for transfers between devices: none -> 19 us  [swap(): return lax.ppermute(x, 'mp', [(0, 1), (1, 0)])]
    unnamed x29 -> x99, local copies, waits for them, and re-layouts: 28.5 us -> 11.3 us
    all_gather x2 -> x0, local copies, waits for them, and re-layouts: 16 us -> none  [encoder(): lax.all_gather(qkv_weight, 'dp', axis=0, tiled=True)]
  transfers between devices with their start and end apart: 16 -> 4, of which waited for: 12 -> 2; matrix products, arithmetic and copies ran while one was open for 13% -> 8% of each run, Pallas kernels for 0% -> 19%
where the time goes in v1:
time: 215 us; the launch traced here: 213 us
  Pallas kernels  149 us (69%)
  local copies, waits for them, and re-layouts  33.7 us (16%)
  waiting for transfers between devices  19 us (9%)
  matrix products  5.77 us (3%)
  starting transfers between devices  3.12 us (1%)
    pallas_call x1, Pallas kernels, gather(): pl.pallas_call(functools.partial(gather_kernel, streams, order), out_shap...  98.3 us
    pallas_call x2, Pallas kernels, mlp(): pl.pallas_call(functools.partial(mlp_kernel, steps, approx, bool(extras))...  27.7 us
    pallas_call x2, Pallas kernels, attention(): pl.pallas_call(functools.partial(attention_kernel, size, at_qkv, n_qkv, a...  23.5 us
    ppermute x4, waiting for transfers between devices, swap(): return lax.ppermute(x, 'mp', [(0, 1), (1, 0)])  19 us
    unnamed x99, local copies, waits for them, and re-layouts  11.3 us
    dot_general x2, matrix products, dot_t(): lax.dot_general(a, b, (((1,), (1,)), ((), ())), preferred_element_type=F32)  4.46 us
  transfers between devices with their start and end apart: 4, of which 2 were waited for; matrix products, arithmetic and copies ran while one was open for 8% of the time, Pallas kernels for 19%

profile of v1, /device:TPU:1, one launch (start us, length us, event | category | flops | bytes accessed | tf_op | source)
XLA Modules:
  0.0 213.0 jit_solution(9204499992946194313)
XLA Ops:
  0.6 0.0 copy-start
  0.9 0.7 slice.99
  1.6 0.7 slice.98
  2.3 0.8 slice.97
  3.1 0.8 slice.96
  3.9 0.8 slice.74
  4.6 0.8 slice.72
  5.4 0.7 slice.79
  6.1 0.8 slice.76
  6.9 0.1 slice.80
  7.1 0.1 pad_reduce_fusion
  7.2 0.1 slice.77
  7.3 0.8 reshape.78
  8.2 0.1 reshape_reshape_reshape.6.refs_1_
  8.4 0.0 copy-start.8
  8.4 0.0 copy-start.9
  8.4 0.8 convolution_convert_fusion.1
  9.2 0.0 copy-start.10
  9.2 0.3 copy.39
  9.6 0.3 copy-done.10
  10.1 0.2 copy-done.36
  10.3 0.5 fusion.19.dino
  10.8 98.3 %gather.1 = (bf16[4,8,2,2,8,14208]{5,4,3,2,1,0:T(8,128)(2,1)S(1)}, bf16[512,512]{1,0:T(8,128)(2,1)S(1)}, bf16[512,576]{1,0:T(8,128)(2,1)S(1)}) custom-call(bf16[8,14208]{1,0:T(8,128)(2,1)S(1)} %constant_dynamic-update-slice_fusion.block, bf16[512,512]{1,0:T(8,128)(2,1)S(1)} %fusion.19.dino, bf16[512,576]{1,0:T(8,128)(2,1)S(1)} %bitcast.32), custom_call_target="tpu_custom_call" | custom-call | flops 1073741824 | bytes 33554432 | tf_op jit(solution)/shard_map/gather/pallas_call | solution.py:177
  109.1 9.6 %copy-done.1 = bf16[4,8,2,2,8,14208]{5,4,3,2,1,0:T(8,128)(2,1)} copy-done((bf16[4,8,2,2,8,14208]{5,4,3,2,1,0:T(8,128)(2,1)}, bf16[4,8,2,2,8,14208]{5,4,3,2,1,0:T(8,128)(2,1)S(1)}, u32[]{:S(2)}) %copy-start.1) | copy-done | bytes 29098008
  118.7 0.1 broadcast_select_fusion.3
  118.7 0.1 pad_maximum_fusion.refs_0_.refs_1_
  118.9 10.5 %attention.2.refs_2_ = bf16[512,1024]{1,0:T(8,128)(2,1)} custom-call(bf16[512,1024]{1,0:T(8,128)(2,1)S(1)} %pad_maximum_fusion.refs_0_.refs_1_, f32[1,1024]{1,0:T(1,128)S(1)} %reshape_reshape_reshape.6.refs_1_, bf16[1024,14208]{1,0:T(8,128)(2,1)} %bitcast.24), custom_call_target="tpu_custom_call" | custom-call | flops 2415919104 | bytes 8388608 | tf_op jit(solution)/shard_map/attention/pallas_call | solution.py:302
  129.5 0.8 collective-permute-start
  130.3 0.1 broadcast_select_fusion
  130.5 0.8 slice.101
  131.3 0.8 slice.100
  132.1 1.2 slice.106
  133.4 0.0 copy-start.11
  133.4 0.4 reshape.85
  133.7 0.0 copy-start.6
  133.8 0.0 copy-start.7
  133.8 0.7 slice.108.refs_4_
  134.5 0.2 reshape.81
  134.8 0.2 slice_reduce_fusion.1
  135.0 0.1 reshape.83
  135.1 1.4 concatenate.25.refs_0_.refs_1_
  136.5 0.9 copy-done.5
  137.4 12.9 %attention.3.refs_2_ = bf16[512,1152]{1,0:T(8,128)(2,1)S(1)} custom-call(bf16[512,1152]{1,0:T(8,128)(2,1)S(1)} %concatenate.25.refs_0_.refs_1_, f32[1,1152]{1,0:T(1,128)S(1)} %reshape.84.refs_1_, bf16[1024,14208]{1,0:T(8,128)(2,1)} %bitcast.26, bf16[128,1792]{1,0:T(8,128)(2,1)S(1)} %slice.107.refs_3_, bf16[128,640]{1,0:T(8,128)(2,1)S(1)} %copy-done.5), custom_call_target="tpu_custom_call" | custom-call | flops 3170893824 | bytes 8388608 | tf_op jit(solution)/shard_map/attention/pallas_call | solution.py:302
  150.4 0.0 copy-start.12
  150.4 1.0 collective-permute-start.2
  151.4 1.4 slice.111
  152.8 0.1 reshape.80
  153.0 0.7 reshape_reshape_reshape.7.refs_4_
  153.7 0.2 reshape.86
  154.0 0.1 reshape.88
  154.1 1.5 reshape.90
  155.6 0.2 slice_reduce_fusion
  155.8 2.3 %fusion.61 = (bf16[128,2304]{1,0:T(8,128)(2,1)}, bf16[128,2304]{1,0:T(8,128)(2,1)}) fusion(bf16[128,5120]{1,0:T(8,128)(2,1)} %reshape.90), kind=kLoop, calls=%fused_computation.138 | loop fusion | bytes 2359296 | tf_op jit(solution)/shard_map/slice | solution.py:493
  158.1 12.7 %mlp.2 = (f32[512,512]{1,0:T(8,128)}, bf16[512,512]{1,0:T(8,128)(2,1)}) custom-call(s32[1]{0:T(128)} %bitcast.refs_0_, bf16[512,1024]{1,0:T(8,128)(2,1)} %copy-done.3, bf16[512,1024]{1,0:T(8,128)(2,1)} %attention.2.refs_2_, bf16[512,1024]{1,0:T(8,128)(2,1)} %collective-permute-done.refs_3_, f32[1,1024]{1,0:T(1,128)} %reshape_reshape_reshape.7.refs_4_, ...), custom_call_target="tpu_custom_call" | custom-call | flops 4294967296 | bytes 12582912 | tf_op jit(solution)/shard_map/mlp/pallas_call | solution.py:403
  170.9 0.6 collective-permute-start.1
  171.5 0.6 reshape.89.refs_4_
  172.1 7.8 %collective-permute-done.2.refs_3_ = bf16[512,1152]{1,0:T(8,128)(2,1)} collective-permute-done((bf16[512,1152]{1,0:T(8,128)(2,1)S(1)}, bf16[512,1152]{1,0:T(8,128)(2,1)}, u32[]{:S(2)}, u32[]{:S(2)}) %collective-permute-start.2) | collective-permute-done | bytes 1179680 | tf_op jit(solution)/shard_map/ppermute | solution.py:236
  179.9 14.9 %mlp.3 = (f32[512,576]{1,0:T(8,128)}, bf16[512,576]{1,0:T(8,128)(2,1)}) custom-call(s32[1]{0:T(128)} %bitcast.refs_0_, bf16[512,1152]{1,0:T(8,128)(2,1)} %copy-done.2, bf16[512,1152]{1,0:T(8,128)(2,1)} %copy-done.4, bf16[512,1152]{1,0:T(8,128)(2,1)} %collective-permute-done.2.refs_3_, f32[1,1152]{1,0:T(1,128)} %reshape.89.refs_4_, ...), custom_call_target="tpu_custom_call" | custom-call | flops 5435817984 | bytes 12582912 | tf_op jit(solution)/shard_map/mlp/pallas_call | solution.py:403
  194.9 1.3 copy.44
  196.2 0.7 collective-permute-start.3
  197.0 1.4 convolution_convert_fusion.2
  198.4 11.1 %collective-permute-done.3 = bf16[512,576]{0,1:T(8,128)(2,1)S(1)} collective-permute-done((bf16[512,576]{0,1:T(8,128)(2,1)S(1)}, bf16[512,576]{0,1:T(8,128)(2,1)S(1)}, u32[]{:S(2)}, u32[]{:S(2)}) %collective-permute-start.3) | collective-permute-done | bytes 589856 | tf_op jit(solution)/shard_map/ppermute | solution.py:236
  209.5 0.3 copy.45
  209.9 3.1 %convolution_convert_fusion = bf16[512,576]{0,1:T(8,128)(2,1)} fusion(f32[512,576]{1,0:T(8,128)} %get-tuple-element.14, bf16[512,576]{1,0:T(8,128)(2,1)S(1)} %copy.45, s32[576]{0:T(1024)S(1)} %get-tuple-element.32, s32[576]{0:T(1024)S(1)} %copy-done.16, s32[576]{0:T(1024)S(1)} %copy-done.18, s32[576]{0:T(1024)S(1)} %copy-done.20, ...), kind=kOutput, calls=%fused_computation.55 | convolution fusion | flops 365469696 | bytes 2372544 | tf_op jit(solution)/shard_map/dot_general | solution.py:250
  (116 shorter events, 0.6 us)
Async XLA Ops:
  0.6 7.7 %copy-start = (bf16[512,576]{0,1:T(8,128)(2,1)S(1)}, bf16[512,576]{0,1:T(8,128)(2,1)}, u32[]{:S(2)}) copy-start(bf16[512,576]{0,1:T(8,128)(2,1)} %param.15) | copy-start | bytes 1769476
  0.7 9.3 %copy-start.43 = (pred[512]{0:T(512)(128)(4,1)}, pred[512]{0:T(512)(128)(4,1)S(1)}, u32[]{:S(2)}) copy-start(pred[512]{0:T(512)(128)(4,1)S(1)} %fusion.56) | copy-start | bytes 1540
  0.7 7.6 %copy-start.37 = (pred[576]{0:T(1024)(128)(4,1)}, pred[576]{0:T(1024)(128)(4,1)S(1)}, u32[]{:S(2)}) copy-start(pred[576]{0:T(1024)(128)(4,1)S(1)} %fusion.49) | copy-start | bytes 1732
  0.7 9.3 %copy-start.39 = (pred[512]{0:T(512)(128)(4,1)}, pred[512]{0:T(512)(128)(4,1)S(1)}, u32[]{:S(2)}) copy-start(pred[512]{0:T(512)(128)(4,1)S(1)} %get-tuple-element.26) | copy-start | bytes 1540
  0.7 9.3 %copy-start.41 = (pred[512]{0:T(512)(128)(4,1)}, pred[512]{0:T(512)(128)(4,1)S(1)}, u32[]{:S(2)}) copy-start(pred[512]{0:T(512)(128)(4,1)S(1)} %get-tuple-element.27) | copy-start | bytes 1540
  0.7 9.3 %copy-start.21 = (s32[512]{0:T(512)}, s32[512]{0:T(512)S(1)}, u32[]{:S(2)}) copy-start(s32[512]{0:T(512)S(1)} %broadcast_add_fusion.1) | copy-start | bytes 6148
  0.8 7.6 %copy-start.31 = (pred[576]{0:T(1024)(128)(4,1)}, pred[576]{0:T(1024)(128)(4,1)S(1)}, u32[]{:S(2)}) copy-start(pred[576]{0:T(1024)(128)(4,1)S(1)} %get-tuple-element.34) | copy-start | bytes 1732
  0.8 7.6 %copy-start.33 = (pred[576]{0:T(1024)(128)(4,1)}, pred[576]{0:T(1024)(128)(4,1)S(1)}, u32[]{:S(2)}) copy-start(pred[576]{0:T(1024)(128)(4,1)S(1)} %get-tuple-element.35) | copy-start | bytes 1732
  0.8 9.2 %copy-start.23 = (s32[512]{0:T(512)}, s32[512]{0:T(512)S(1)}, u32[]{:S(2)}) copy-start(s32[512]{0:T(512)S(1)} %get-tuple-element.24) | copy-start | bytes 6148
  0.8 9.2 %copy-start.25 = (s32[512]{0:T(512)}, s32[512]{0:T(512)S(1)}, u32[]{:S(2)}) copy-start(s32[512]{0:T(512)S(1)} %get-tuple-element.25) | copy-start | bytes 6148
  0.8 9.2 %copy-start.27 = (s32[512]{0:T(512)}, s32[512]{0:T(512)S(1)}, u32[]{:S(2)}) copy-start(s32[512]{0:T(512)S(1)} %get-tuple-element.22) | copy-start | bytes 6148
  0.8 9.2 %copy-start.29 = (s32[512]{0:T(512)}, s32[512]{0:T(512)S(1)}, u32[]{:S(2)}) copy-start(s32[512]{0:T(512)S(1)} %get-tuple-element.23) | copy-start | bytes 6148
  0.9 7.5 %copy-start.15 = (s32[576]{0:T(1024)}, s32[576]{0:T(1024)S(1)}, u32[]{:S(2)}) copy-start(s32[576]{0:T(1024)S(1)} %get-tuple-element.33) | copy-start | bytes 6916
  0.9 7.5 %copy-start.17 = (s32[576]{0:T(1024)}, s32[576]{0:T(1024)S(1)}, u32[]{:S(2)}) copy-start(s32[576]{0:T(1024)S(1)} %get-tuple-element.30) | copy-start | bytes 6916
  0.9 7.5 %copy-start.19 = (s32[576]{0:T(1024)}, s32[576]{0:T(1024)S(1)}, u32[]{:S(2)}) copy-start(s32[576]{0:T(1024)S(1)} %get-tuple-element.31) | copy-start | bytes 6916
  8.4 1.2 copy-start.8
  8.4 1.2 copy-start.9
  9.2 0.7 copy-start.10
  9.2 0.7 copy-start.13
  9.2 1.1 copy-start.36
  109.1 9.6 %copy-start.1 = (bf16[4,8,2,2,8,14208]{5,4,3,2,1,0:T(8,128)(2,1)}, bf16[4,8,2,2,8,14208]{5,4,3,2,1,0:T(8,128)(2,1)S(1)}, u32[]{:S(2)}) copy-start(bf16[4,8,2,2,8,14208]{5,4,3,2,1,0:T(8,128)(2,1)S(1)} %get-tuple-element.10) | copy-start | bytes 87293952
  118.9 10.6 %copy-start.3 = (bf16[512,1024]{1,0:T(8,128)(2,1)}, bf16[512,1024]{1,0:T(8,128)(2,1)S(1)}, u32[]{:S(2)}) copy-start(bf16[512,1024]{1,0:T(8,128)(2,1)S(1)} %pad_maximum_fusion.refs_0_.refs_1_) | copy-start | bytes 3145732
  129.5 28.7 %collective-permute-start = (bf16[512,1024]{1,0:T(8,128)(2,1)}, bf16[512,1024]{1,0:T(8,128)(2,1)}, u32[]{:S(2)}, u32[]{:S(2)}) collective-permute-start(bf16[512,1024]{1,0:T(8,128)(2,1)} %attention.2.refs_2_), channel_id=1, source_target_pairs={{0,1},{1,0},{2,3},{3,2},{4,5},{5,4},{6,7},{7,6},{8,9},{9,8},{10,11... | collective-permute-start | bytes 3145736 | tf_op jit(solution)/shard_map/ppermute | solution.py:236
  133.4 1.1 copy-start.11
  133.7 1.4 copy-start.6
  133.8 1.4 copy-start.7
  136.5 0.9 copy-start.5
  137.4 12.9 %copy-start.2 = (bf16[512,1152]{1,0:T(8,128)(2,1)}, bf16[512,1152]{1,0:T(8,128)(2,1)S(1)}, u32[]{:S(2)}) copy-start(bf16[512,1152]{1,0:T(8,128)(2,1)S(1)} %concatenate.25.refs_0_.refs_1_) | copy-start | bytes 3538948
  150.4 3.6 %copy-start.4 = (bf16[512,1152]{1,0:T(8,128)(2,1)}, bf16[512,1152]{1,0:T(8,128)(2,1)S(1)}, u32[]{:S(2)}) copy-start(bf16[512,1152]{1,0:T(8,128)(2,1)S(1)} %attention.3.refs_2_) | copy-start | bytes 3538948
  150.4 2.4 %copy-start.14 = (f32[1024]{0:T(1024)S(1)}, f32[1024]{0:T(1024)}, u32[]{:S(2)}) copy-start(f32[1024]{0:T(1024)} %param.19) | copy-start | bytes 12292
  150.4 3.4 %copy-start.12 = (f32[1152]{0:T(1024)S(1)}, f32[1152]{0:T(1024)}, u32[]{:S(2)}) copy-start(f32[1152]{0:T(1024)} %param.25) | copy-start | bytes 13828
  150.4 29.5 %collective-permute-start.2 = (bf16[512,1152]{1,0:T(8,128)(2,1)S(1)}, bf16[512,1152]{1,0:T(8,128)(2,1)}, u32[]{:S(2)}, u32[]{:S(2)}) collective-permute-start(bf16[512,1152]{1,0:T(8,128)(2,1)S(1)} %attention.3.refs_2_), channel_id=1, source_target_pairs={{0,1},{1,0},{2,3},{3,2},{4,5},{5,4},{6,7},{7,6},{8,9},{9,8},{10,11... | collective-permute-start | bytes 3538952 | tf_op jit(solution)/shard_map/ppermute | solution.py:236
  170.9 26.0 %collective-permute-start.1 = (bf16[512,512]{1,0:T(8,128)(2,1)}, bf16[512,512]{1,0:T(8,128)(2,1)S(1)}, u32[]{:S(2)}, u32[]{:S(2)}) collective-permute-start(bf16[512,512]{1,0:T(8,128)(2,1)} %get-tuple-element.12), channel_id=1, source_target_pairs={{0,1},{1,0},{2,3},{3,2},{4,5},{5,4},{6,7},{7,6},{8,9},{9,8},{10,11... | collective-permute-start | bytes 1572872 | tf_op jit(solution)/shard_map/ppermute | solution.py:236
  179.9 17.0 %copy-start.22 = (s32[512]{0:T(512)S(1)}, s32[512]{0:T(512)}, u32[]{:S(2)}) copy-start(s32[512]{0:T(512)} %copy-done.21) | copy-start | bytes 6148
  179.9 17.0 %copy-start.24 = (s32[512]{0:T(512)S(1)}, s32[512]{0:T(512)}, u32[]{:S(2)}) copy-start(s32[512]{0:T(512)} %copy-done.23) | copy-start | bytes 6148
  179.9 17.0 %copy-start.26 = (s32[512]{0:T(512)S(1)}, s32[512]{0:T(512)}, u32[]{:S(2)}) copy-start(s32[512]{0:T(512)} %copy-done.25) | copy-start | bytes 6148
  179.9 17.0 %copy-start.28 = (s32[512]{0:T(512)S(1)}, s32[512]{0:T(512)}, u32[]{:S(2)}) copy-start(s32[512]{0:T(512)} %copy-done.27) | copy-start | bytes 6148
  179.9 17.0 %copy-start.30 = (s32[512]{0:T(512)S(1)}, s32[512]{0:T(512)}, u32[]{:S(2)}) copy-start(s32[512]{0:T(512)} %copy-done.29) | copy-start | bytes 6148
  179.9 17.0 %copy-start.35 = (f32[512,512]{1,0:T(8,128)S(1)}, f32[512,512]{1,0:T(8,128)}, u32[]{:S(2)}) copy-start(f32[512,512]{1,0:T(8,128)} %get-tuple-element.11) | copy-start | bytes 3145732
  179.9 17.0 %copy-start.40 = (pred[512]{0:T(512)(128)(4,1)S(1)}, pred[512]{0:T(512)(128)(4,1)}, u32[]{:S(2)}) copy-start(pred[512]{0:T(512)(128)(4,1)} %copy-done.39) | copy-start | bytes 1540
  179.9 17.0 %copy-start.42 = (pred[512]{0:T(512)(128)(4,1)S(1)}, pred[512]{0:T(512)(128)(4,1)}, u32[]{:S(2)}) copy-start(pred[512]{0:T(512)(128)(4,1)} %copy-done.41) | copy-start | bytes 1540
  179.9 17.0 %copy-start.44 = (pred[512]{0:T(512)(128)(4,1)S(1)}, pred[512]{0:T(512)(128)(4,1)}, u32[]{:S(2)}) copy-start(pred[512]{0:T(512)(128)(4,1)} %copy-done.43) | copy-start | bytes 1540
  196.2 13.3 %collective-permute-start.3 = (bf16[512,576]{0,1:T(8,128)(2,1)S(1)}, bf16[512,576]{0,1:T(8,128)(2,1)S(1)}, u32[]{:S(2)}, u32[]{:S(2)}) collective-permute-start(bf16[512,576]{0,1:T(8,128)(2,1)S(1)} %copy.44), channel_id=1, source_target_pairs={{0,1},{1,0},{2,3},{3,2},{4,5},{5,4},{6,7},{7,6},{8,9},{9,8},{10,11... | collective-permute-start | bytes 1769480 | tf_op jit(solution)/shard_map/ppermute | solution.py:236
  197.0 12.8 %copy-start.16 = (s32[576]{0:T(1024)S(1)}, s32[576]{0:T(1024)}, u32[]{:S(2)}) copy-start(s32[576]{0:T(1024)} %copy-done.15) | copy-start | bytes 6916
  197.0 12.8 %copy-start.18 = (s32[576]{0:T(1024)S(1)}, s32[576]{0:T(1024)}, u32[]{:S(2)}) copy-start(s32[576]{0:T(1024)} %copy-done.17) | copy-start | bytes 6916
  197.0 12.8 %copy-start.20 = (s32[576]{0:T(1024)S(1)}, s32[576]{0:T(1024)}, u32[]{:S(2)}) copy-start(s32[576]{0:T(1024)} %copy-done.19) | copy-start | bytes 6916
  197.0 12.8 %copy-start.32 = (pred[576]{0:T(1024)(128)(4,1)S(1)}, pred[576]{0:T(1024)(128)(4,1)}, u32[]{:S(2)}) copy-start(pred[576]{0:T(1024)(128)(4,1)} %copy-done.31) | copy-start | bytes 1732
  197.0 12.8 %copy-start.34 = (pred[576]{0:T(1024)(128)(4,1)S(1)}, pred[576]{0:T(1024)(128)(4,1)}, u32[]{:S(2)}) copy-start(pred[576]{0:T(1024)(128)(4,1)} %copy-done.33) | copy-start | bytes 1732
  197.0 12.8 %copy-start.38 = (pred[576]{0:T(1024)(128)(4,1)S(1)}, pred[576]{0:T(1024)(128)(4,1)}, u32[]{:S(2)}) copy-start(pred[576]{0:T(1024)(128)(4,1)} %copy-done.37) | copy-start | bytes 1732

commit v2 on v0

v2 whole, which is shorter than its diff:
```python
import functools
import heapq
import math

import jax
import jax.numpy as jnp
from jax import lax
from jax.experimental import pallas as pl
from jax.experimental.pallas import tpu as pltpu
from jax.sharding import PartitionSpec as P

HEADS = 16
LOCAL = HEADS // 2
PATCHES = 256
EPS = 1e-06
BF = jnp.bfloat16
F32 = jnp.float32

Y, XH, Z, C = 4, 2, 8, 2


RING = {"y": Y, "z": Z}


def onward(order, piece):
    dy, dz, dx, half = piece
    place = {"y": dy, "z": dz}

    def ring(axis):
        d, n = place[axis], RING[axis]

        def at(to, h):
            spot = dict(place, **{axis: to})
            return (spot["y"], spot["z"], dx, h)

        if d == 0:
            return [(axis + "+", at(-1, half)), (axis + "-", at(1, half))]
        if d < 0 and -d < n // 2 - 1:
            return [(axis + "+", at(d - 1, half))]
        if d > 0 and d < n // 2 - 1:
            return [(axis + "-", at(d + 1, half))]
        if d == 1 - n // 2 and half != 1:
            return [(axis + "+", at(-n // 2, 0))]
        if d == n // 2 - 1 and half != 0:
            return [(axis + "-", at(-n // 2, 1))]
        return []

    first, second = order
    sends = ring(first) if place[second] == 0 else []
    return sends + ring(second)


def schedule(streams, tasks, rate=0.05, hop=2.5, across=10.0, issue=0.08, shallow=1.5, deep=10.0):
    free = dict.fromkeys(("y+", "y-", "z+", "z-"), 0.0)
    pending = {link: [] for link in free}
    coming, program, count, now, done = [], [], 0, 0.0, 0
    for s in range(len(streams)):
        heapq.heappush(coming, (0.0, count, s, (0, 0, 0, None)))
        heapq.heappush(coming, (across, count + 1, s, (0, 0, 1, None)))
        count += 2
    first = [s for s, stream in enumerate(streams) if stream[3] == 0]
    left = sum(1 for s in first for _ in range(2 * 43))
    complete = None
    while coming or any(pending.values()):
        task = tasks[done] if done < len(tasks) else None
        ready = task is not None and now >= task[0] and (not task[1] or (complete is not None and now >= complete + 3.0))
        depth = deep if complete is not None and task is not None else shallow
        for link, queue in pending.items():
            while queue and free[link] - now < depth:
                _, _, s, piece, child = heapq.heappop(queue)
                program.append(("send", s, piece, link, child))
                now += issue
                size = streams[s][2] * (1.0 if child[3] is None else 0.5)
                free[link] = max(free[link], now) + size * rate
                count += 1
                heapq.heappush(coming, (free[link] + hop, count, s, child))
        if ready:
            slack = [free[link] - now for link in free]
            if sum(min(x, task[2]) for x in slack) >= 0.55 * 4 * task[2] or not coming or coming[0][0] > now + 1.0:
                program.append(("task", done))
                now += task[2]
                done += 1
                continue
        if not coming:
            now += 0.2
            continue
        t, _, s, piece = heapq.heappop(coming)
        now = max(now, t) + issue
        program.append(("wait", s, piece))
        if s in first:
            left -= 1
            if left == 0:
                complete = now
        for link, child in onward(streams[s][0], piece):
            count += 1
            heapq.heappush(pending[link], (streams[s][3], count, s, piece, child))
    comm = now
    for k in range(done, len(tasks)):
        program.append(("task", k))
        now += tasks[k][2]
    return program, complete, comm, now


TASKS = [(0.0, False, 2.0), (30.0, False, 1.5), (0.0, True, 0.5), (0.0, True, 1.0)]
TASKS += [(0.0, True, d) for d in (2.5, 2.6, 1.6) * 2] + [(40.0, True, 1.2)] + [(0.0, True, d) for d in (2.2, 2.0, 1.2) * 2]
UP_S, UP_D, REST_TWO, QKV_D, OUT_D, QKV_S, OUT_S, REST_ONE, END = 0, 4608, 8704, 9344, 10880, 11392, 13184, 13824, 14208


def layer_kernel(
    streams, program, d_qkv, d_out, d_up, d_down, s_qkv, s_out, s_up, s_down, dino, siglip, dino_one, dino_two, siglip_one, siglip_two, dino_out, siglip_out,
    send, recv, pass_send, pass_recv, more_send, more_recv,
    w, dino_x, siglip_x, dino_part, siglip_part, dino_got, siglip_got, dino_gain, siglip_gain,
    block, dino_in, siglip_in, hot_d, hot_s, rest_q, rest_o, qkv_buf, ctx_buf,
    rest_two, second, acc, keep_d, keep_s, sent_d, sent_s, back_d, back_s,
):
    me, mp = lax.axis_index("dp"), lax.axis_index("mp")
    c, z, xh, y = lax.rem(me, 2), lax.rem(me // 2, 8), lax.rem(me // 16, 2), me // 32
    low = mp == 0

    def at(y, xh, z, c):
        return ((y * XH + xh) * Z + z) * C + c

    up_y, down_y = lax.rem(y + 1, Y), lax.rem(y + Y - 1, Y)
    up_z, down_z = lax.rem(z + 1, Z), lax.rem(z + Z - 1, Z)
    to = {
        "y+": (at(up_y, xh, z, c), mp),
        "y-": (at(down_y, xh, z, c), mp),
        "z+": (at(y, xh, up_z, c), mp),
        "z-": (at(y, xh, down_z, c), mp),
        "x": (at(y, 1 - xh, z, c), mp),
        "core": (at(y, xh, z, 1 - c), mp),
        "mp": (me, 1 - mp),
    }
    timeline = [step[1:] for step in program if step[0] == "wait"]
    number = {event: i for i, event in enumerate(timeline)}

    def columns(s, half):
        _, start, tiles, _ = streams[s]
        first, last = {None: (0, tiles), 0: (0, tiles // 2), 1: (tiles // 2, tiles)}[half]
        return slice((start + first) * 128, (start + last) * 128)

    def spot(s, piece, half=None, core=None):
        dy, dz, dx, mine = piece
        half = mine if half is None else half
        source = (lax.rem(y + dy + Y, Y), lax.rem(z + dz + Z, Z), c if core is None else core, lax.rem(xh + dx, 2))
        return w.at[(*source, slice(None), columns(s, half))]

    def remote(src, dst, sends, receives, k, link):
        return pltpu.make_async_remote_copy(
            src_ref=src,
            dst_ref=dst,
            send_sem=sends.at[k],
            recv_sem=receives.at[k],
            device_id=to[link],
            device_id_type=pl.DeviceIdType.MESH,
        )

    def source_of(s, piece, half):
        if piece[:3] == (0, 0, 0):
            return block.at[:, columns(s, half)]
        return spot(s, piece, half)

    def hop(s, piece, link, child):
        return remote(source_of(s, piece, child[3]), spot(s, piece, child[3]), send, recv, number[(s, child)], link)

    def share(s, piece):
        return remote(source_of(s, piece, piece[3]), spot(s, piece), pass_send, pass_recv, number[(s, piece)], "core")

    def arrived(s, piece):
        return remote(spot(s, piece), spot(s, piece), send, recv, number[(s, piece)], "y+")

    def shared(s, piece):
        there = spot(s, piece, core=1 - c)
        return remote(there, there, pass_send, pass_recv, number[(s, piece)], "core")

    barrier = pltpu.get_barrier_semaphore()
    for device in to.values():
        pl.semaphore_signal(barrier, inc=1, device_id=device, device_id_type=pl.DeviceIdType.MESH)
    for start, width, mine in ((UP_S, 2304, s_up), (UP_S + 2304, 2304, s_down), (QKV_S, 1792, s_qkv), (OUT_S, 640, s_out)):
        got = mine.shape[1]
        block[:, start : start + got] = mine[:8, :]
        block[:, start + got : start + width] = jnp.zeros((8, width - got), BF)
    for i in range(3):
        block[:, QKV_D + i * 512 : QKV_D + (i + 1) * 512] = d_qkv[i]
    block[:, OUT_D:QKV_S] = d_out[...]
    block[:, UP_D : UP_D + 2048] = d_up[...]
    block[:, UP_D + 2048 : REST_TWO] = d_down[...]
    for start, width, mine in ((REST_ONE, 384, ((s_qkv, 1792), (s_out, 640))), (REST_TWO, 640, ((s_up, 2304), (s_down, 2304)))):
        ninth, long = [], 8 * width
        for ref, to_width in mine:
            ninth += [ref[8:9, :], jnp.zeros((1, to_width - ref.shape[1]), BF)]
            long -= to_width
        ninth = jnp.concatenate([*ninth, jnp.zeros((1, long), BF)], axis=1)
        for r in range(8):
            block[r : r + 1, start : start + width] = ninth[:, r * width : (r + 1) * width]
    pl.semaphore_wait(barrier, len(to))

    across = [hop(s, (0, 0, 0, None), "x", (0, 0, 1, None)) for s in range(len(streams))]
    tokens_s = remote(siglip, siglip_in, more_send, more_recv, 0, "mp")
    tokens_d = remote(dino, dino_in, more_send, more_recv, 1, "mp")
    for copy in across:
        copy.start()
    tokens_s.start()
    tokens_d.start()
    started, parts = list(across), []

    def matrix(start, stop):
        return w[:, :, :, :, :, start:stop].reshape(1024, stop - start)

    def chosen(r):
        rows, columns = (lax.broadcasted_iota(jnp.int32, (128, 1024), axis) for axis in range(2))
        return (columns == rows * 8 + r).astype(BF)

    def begin():
        w[y, z, c, xh] = block[...]
        hot_d[...] = one_hot(8)
        hot_s[...] = one_hot(9)
        for one, two, hot, out in ((dino_one, dino_two, hot_d, dino_gain), (siglip_one, siglip_two, hot_s, siglip_gain)):
            half = hot.shape[0]
            gains = jnp.concatenate([one[:, :half], two[:, :half], one[:, half:], two[:, half:]], axis=0)
            held = jnp.dot(gains, hot[...].astype(F32), preferred_element_type=F32, precision=lax.Precision.HIGHEST)
            out[:, :512], out[:, 512:1024] = held[0:2, :512], held[2:4, :512]
            if out.shape[1] > 1024:
                out[:, 1024:1088], out[:, 1088:] = held[0:2, 512:], held[2:4, 512:]

    def pick(ref, rows, hot):
        if ref.shape[0] == hot.shape[0] and ref.shape[1] != hot.shape[0]:
            return lax.dot_general(ref[:, rows], hot[...], (((0,), (0,)), ((), ())), preferred_element_type=F32).astype(BF)
        return dot(ref[rows, :], hot[...]).astype(BF)

    def place(ref, other, hot, out, copy):
        def go():
            copy.wait_recv()
            for i in range(2):
                rows = slice(i * 256, (i + 1) * 256)
                held, far = pick(ref, rows, hot), pick(other, rows, hot)
                first, second = jnp.where(low, held, far), jnp.where(low, far, held)
                out[rows, :512], out[rows, 512:1024] = first[:, :512], second[:, :512]
                if out.shape[1] > 1024:
                    out[rows, 1024:] = jnp.concatenate([first[:, 512:], second[:, 512:]], axis=1)

        return go

    early = [s for s, stream in enumerate(streams) if stream[3] == 0]

    def load():
        for s, piece in timeline:
            if s in early:
                shared(s, piece).wait_recv()

    def ready_s():
        block_rest = matrix(REST_ONE, END)
        for r in range(8):
            got = dot(chosen(r), block_rest).astype(BF)
            start = r * 384
            if start + 384 <= 1792:
                rest_q[:, start : start + 384] = got
            elif start < 1792:
                rest_q[:, start:] = got[:, : 1792 - start]
                rest_o[:, : start + 384 - 1792] = got[:, 1792 - start :]
            elif start < 2432:
                stop = min(start + 384, 2432)
                rest_o[:, start - 1792 : stop - 1792] = got[:, : stop - start]

    def project(x, gain, wq, more, n):
        def go(f):
            rows = slice(f * PATCHES, (f + 1) * PATCHES)
            v = normed(x[rows, :].astype(F32), gain[0:1, :])
            qkv = dot(v[:, :1024], matrix(*wq))
            if more is not None:
                qkv = qkv + dot(v[:, 1024:], more[...])
            qkv_buf[:, :n] = qkv.astype(BF)

        return go

    def attend(size, n):
        def go(f):
            scale, held = 1.0 / math.sqrt(size), LOCAL * size
            qkv = qkv_buf[:, : 3 * held]
            heads = []
            for h in range(LOCAL):
                q, k, v = (qkv[:, j * held + h * size : j * held + (h + 1) * size] for j in range(3))
                s = dot_t(q, k)
                e = jnp.exp((s - jnp.max(s, axis=-1, keepdims=True)) * scale)
                total = jnp.sum(e, axis=-1, keepdims=True)
                heads.append((dot(e.astype(BF), v) / total).astype(BF))
            if n > held:
                heads.append(jnp.zeros((PATCHES, n - held), BF))
            ctx_buf[:, :n] = jnp.concatenate(heads, axis=1)

        return go

    def leave(wo, more, n, part, got, k):
        def go(f):
            rows = slice(f * PATCHES, (f + 1) * PATCHES)
            ctx = ctx_buf[:, :n]
            part[rows, :1024] = dot_t(ctx, matrix(*wo)).astype(BF)
            if more is not None:
                part[rows, 1024:] = dot_t(ctx, more[...]).astype(BF)
            parts.append(remote(part.at[rows], got.at[rows], more_send, more_recv, k + f, "mp"))

        return go

    steps_s = [project(siglip_x, siglip_gain, (QKV_S, OUT_S), rest_q, 1792), attend(72, 640), leave((OUT_S, REST_ONE), rest_o, 640, siglip_part, siglip_got, 2)]
    steps_d = [project(dino_x, dino_gain, (QKV_D, OUT_D), None, 1536), attend(64, 512), leave((OUT_D, QKV_S), None, 512, dino_part, dino_got, 4)]
    work = [begin, place(siglip, siglip_in, hot_s, siglip_x, tokens_s), load, ready_s]
    work += [functools.partial(go, f) for f in range(2) for go in steps_s]
    work += [place(dino, dino_in, hot_d, dino_x, tokens_d)]
    work += [functools.partial(go, f) for f in range(2) for go in steps_d]

    sent = 0
    for kind, *step in program:
        while sent < len(parts):
            parts[sent].start()
            sent += 1
        if kind == "task":
            work[step[0]]()
        elif kind == "send":
            s, piece, link, child = step
            started.append(hop(s, piece, link, child))
            started[-1].start()
        else:
            s, piece = step
            if piece[:3] != (0, 0, 0):
                arrived(s, piece).wait_recv()
            share(s, piece).start()
    while sent < len(parts):
        parts[sent].start()
        sent += 1
    for copy in started:
        copy.wait_send()
    for s, piece in timeline:
        share(s, piece).wait_send()
        if s not in early:
            shared(s, piece).wait_recv()
    tokens_s.wait_send()
    tokens_d.wait_send()
    for copy in parts:
        copy.wait()

    for r in range(8):
        rest_two[:, r * 640 : (r + 1) * 640] = dot(chosen(r), matrix(REST_TWO, QKV_D)).astype(BF)

    def columns(start, j, chunk):
        return pl.ds(pl.multiple_of(start + j * chunk, 128), chunk)

    def mlp(x, part, got, gain, at, chunk, steps, approx, keep, out, back, k):
        extra = x.shape[1] > 1024

        def rows_of(i, carry):
            rows = pl.ds(pl.multiple_of(i * 256, 256), 256)
            m = x[rows, :].astype(F32) + (part[rows, :].astype(F32) + got[rows, :].astype(F32))
            m = m.astype(BF)
            x[rows, :] = m
            second[:, : x.shape[1]] = normed(m.astype(F32), gain[1:2, :])
            acc[...] = jnp.zeros_like(acc)

            def chunk_of(j, carry):
                up = w[:, :, :, :, :, columns(at, j, chunk)].reshape(1024, chunk)
                down = w[:, :, :, :, :, columns(at + steps * chunk, j, chunk)].reshape(1024, chunk)
                raised = dot(second[:, :1024], up)
                if extra:
                    raised = raised + dot(second[:, 1024:], rest_two[:, columns(0, j, chunk)])
                hidden = gelu(raised, approx).astype(BF)
                acc[:, :1024] += dot_t(hidden, down)
                if extra:
                    acc[:, 1024:] += dot_t(hidden, rest_two[:, columns(steps * chunk, j, chunk)])
                return carry

            lax.fori_loop(0, steps, chunk_of, 0)

            def put(keep_at, send_at):
                keep[rows, :512] = x[rows, keep_at : keep_at + 512].astype(F32) + acc[:, keep_at : keep_at + 512]
                out[rows, :512] = acc[:, send_at : send_at + 512].astype(BF)
                if extra:
                    ka, sa = 1024 + keep_at // 8, 1024 + send_at // 8
                    keep[rows, 512:] = x[rows, ka : ka + 64].astype(F32) + acc[:, ka : ka + 64]
                    out[rows, 512:] = acc[:, sa : sa + 64].astype(BF)

            @pl.when(low)
            def _():
                put(0, 512)

            @pl.when(jnp.logical_not(low))
            def _():
                put(512, 0)

            remote(out.at[rows], back.at[rows], more_send, more_recv, k + i, "mp").start()
            return carry

        lax.fori_loop(0, 2, rows_of, 0)

    mlp(siglip_x, siglip_part, siglip_got, siglip_gain, UP_S, 768, 3, True, keep_s, sent_s, back_s, 6)
    mlp(dino_x, dino_part, dino_got, dino_gain, UP_D, 512, 4, False, keep_d, sent_d, back_d, 8)
    for keep, out, back, k in ((keep_s, sent_s, back_s, 6), (keep_d, sent_d, back_d, 8)):
        for i in range(2):
            rows = slice(i * 256, (i + 1) * 256)
            remote(out.at[rows], back.at[rows], more_send, more_recv, k + i, "mp").wait()
            result = (keep[rows, :] + back[rows, :].astype(F32)).astype(BF)
            if k == 6:
                siglip_out[:, rows] = dot_t(hot_s[...], result).astype(BF)
            else:
                dino_out[rows, :] = dot_t(result, hot_d[...]).astype(BF)


def layer(shards, dino, siglip, *gains):
    streams = (
        ("yz", QKV_D // 128, 13, 0),
        ("zy", QKV_D // 128 + 13, 25, 0),
        ("yz", 0, 28, 1),
        ("zy", 28, 45, 1),
    )
    program = schedule(streams, TASKS)[0]
    vmem = pl.BlockSpec(memory_space=pltpu.VMEM)
    dma = pltpu.SemaphoreType.DMA
    n = sum(step[0] == "wait" for step in program)
    rows = dino.shape[0]
    wide = lambda width, height=rows, dtype=BF: pltpu.VMEM((height, width), dtype)
    return pl.pallas_call(
        functools.partial(layer_kernel, streams, program),
        out_shape=(jax.ShapeDtypeStruct(dino.shape, BF), jax.ShapeDtypeStruct(siglip.shape, BF)),
        in_specs=[vmem] * 14,
        out_specs=(vmem, vmem),
        scratch_shapes=[
            dma((n,)), dma((n,)), dma((n,)), dma((n,)), dma((10,)), dma((10,)),
            pltpu.VMEM((Y, Z, C, XH, 8, END), BF),
            wide(1024), wide(1152), wide(1024), wide(1152), wide(1024), wide(1152), wide(1024, 2, F32), wide(1152, 2, F32),
            wide(END, 8), wide(512), pltpu.VMEM(siglip.shape, BF), wide(512, 512), wide(576, 576),
            wide(1792, 128), wide(640, 128), wide(1792, PATCHES), wide(640, PATCHES),
            wide(5120, 128), wide(1152, 256), wide(1152, 256, F32),
            wide(512, rows, F32), wide(576, rows, F32), wide(512), wide(576), wide(512), wide(576),
        ],
        compiler_params=pltpu.CompilerParams(
            collective_id=0, has_side_effects=True, vmem_limit_bytes=67043328
        ),
        cost_estimate=pl.CostEstimate(flops=1 << 34, bytes_accessed=32 << 20, transcendentals=1 << 22),
        name="layer",
    )(*shards, dino, siglip, *gains)


def one_hot(per_device):
    width = 64 * per_device
    held = lax.broadcasted_iota(jnp.int32, (width, width), 1)
    slot = jnp.where(held < 512, held // 8, held - 512)
    row = jnp.where(held < 512, held % 8, 8)
    xh, c, z, y = slot % 2, (slot // 2) % 2, (slot // 4) % 8, slot // 32
    natural = (((y * XH + xh) * Z + z) * C + c) * per_device + row
    return (lax.broadcasted_iota(jnp.int32, (width, width), 0) == natural).astype(BF)


def normed(x, gain):
    center = x - jnp.mean(x, axis=-1, keepdims=True)
    spread = jnp.mean(center * center, axis=-1, keepdims=True)
    return (center * lax.rsqrt(spread + EPS) * gain).astype(BF)


def dot(a, b):
    return jnp.dot(a, b, preferred_element_type=F32)


def dot_t(a, b):
    return lax.dot_general(a, b, (((1,), (1,)), ((), ())), preferred_element_type=F32)


def gelu(x, approx):
    if approx:
        return jax.nn.gelu(x, approximate=True)
    half = 0.5 * x
    return half + half * lax.erf(x * math.sqrt(0.5))


def local(
    dino_tokens,
    siglip_tokens,
    dino_norm_one,
    dino_qkv,
    dino_out,
    dino_norm_two,
    dino_up,
    dino_down,
    siglip_norm_one,
    siglip_qkv,
    siglip_out,
    siglip_norm_two,
    siglip_up,
    siglip_down,
):
    shards = [
        dino_qkv.transpose(1, 0, 2), dino_out.T, dino_up, dino_down.T,
        siglip_qkv.reshape(9, -1), siglip_out.T, siglip_up, siglip_down.T,
    ]
    gains = [g.reshape(1, -1) for g in (dino_norm_one, dino_norm_two, siglip_norm_one, siglip_norm_two)]
    dino_result, siglip_result = layer(shards, dino_tokens, siglip_tokens.T, *gains)
    return (dino_result, siglip_result.T)


def solution(mesh):
    in_specs = (
        P("dp", "mp"),
        P("dp", "mp"),
        P(),
        P("dp", None, "mp"),
        P("mp", "dp"),
        P(),
        P("dp", "mp"),
        P("mp", "dp"),
        P(),
        P("dp", None, "mp"),
        P("mp", "dp"),
        P(),
        P("dp", "mp"),
        P("mp", "dp"),
    )
    out_specs = (P("dp", "mp"), P("dp", "mp"))
    return jax.shard_map(local, mesh=mesh, in_specs=in_specs, out_specs=out_specs, check_vma=False)
```

time: 1030 us -> 162 us (0.16)
  waiting for transfers between devices: 842 us -> 0 us
  Pallas kernels: 0 us -> 155 us
  local copies, waits for them, and re-layouts: 71.3 us -> 6.14 us
  matrix products: 46.9 us -> 0 us
  starting transfers between devices: 30.4 us -> 0 us
  other arithmetic: 18.8 us -> 0 us
  between operations: 14.9 us -> 0.67 us
    all_gather x8 -> x0, waiting for transfers between devices: 788 us -> none  [the longest x2 242 us: encoder(): lax.all_gather(down_weight, 'dp', axis=1, tiled=True)]
    pallas_call x0 -> x1, Pallas kernels: none -> 155 us  [layer(): pl.pallas_call(functools.partial(layer_kernel, streams, program), out_sha...]
    all_to_all x8 -> x0, waiting for transfers between devices: 49.7 us -> none  [the longest x4 38.1 us: sum_at_owner(): lax.all_to_all(pieces, axis, split_axis=0, concat_axis=0, tiled=True)]
    dot_general x10 -> x0, matrix products: 46.9 us -> none  [the longest x2 30.2 us: encoder(): jnp.dot(hidden, lax.all_gather(down_weight, 'dp', axis=1, tiled=True), pr...]
    all_to_all x8 -> x0, starting transfers between devices: 30.1 us -> none  [the longest x4 15.4 us: sum_at_owner(): lax.all_to_all(pieces, axis, split_axis=0, concat_axis=0, tiled=True)]
    unnamed x29 -> x8, local copies, waits for them, and re-layouts: 28.5 us -> 3.43 us
    all_gather x2 -> x0, local copies, waits for them, and re-layouts: 16 us -> none  [encoder(): lax.all_gather(qkv_weight, 'dp', axis=0, tiled=True)]
  transfers between devices with their start and end apart: 16 -> 0, of which waited for: 12 -> 0; matrix products, arithmetic and copies ran while one was open for 13% -> 0% of each run, Pallas kernels for 0% -> 0%
where the time goes in v2:
time: 162 us
  Pallas kernels  155 us (96%)
  local copies, waits for them, and re-layouts  6.14 us (4%)
    pallas_call x1, Pallas kernels, layer(): pl.pallas_call(functools.partial(layer_kernel, streams, program), out_sha...  155 us
    unnamed x8, local copies, waits for them, and re-layouts  3.43 us

profile of v2, /device:TPU:1, one launch (start us, length us, event | category | flops | bytes accessed | tf_op | source)
XLA Modules:
  0.0 161.8 jit_solution(220824102110182934)
XLA Ops:
  0.6 0.0 copy-start.1
  0.6 0.0 copy-start.2
  0.6 0.7 copy-done.1
  1.3 0.6 reshape.22.siglip_one
  1.9 0.0 copy-done.2
  1.9 0.6 reshape.23.siglip_two
  2.5 1.5 reshape.19.s_qkv
  4.0 155.0 %layer.1 = (bf16[512,512]{1,0:T(8,128)(2,1)}, bf16[576,512]{1,0:T(8,128)(2,1)}) custom-call(bf16[3,8,512]{2,1,0:T(8,128)(2,1)} %bitcast.13, bf16[8,512]{1,0:T(8,128)(2,1)} %bitcast.15, bf16[8,2048]{1,0:T(8,128)(2,1)} %d_up.1, bf16[8,2048]{1,0:T(8,128)(2,1)} %bitcast.12, bf16[9,1728]{1,0:T(8,128)(2,1)} %reshape.19.s_qkv, bf16[9,576]{1,0:T(8,128)(2,1)} %bitcast.14, ...), custom_call_target="tpu_custom_call" | custom-call | flops 17179869184 | bytes 33554432 | tf_op jit(solution)/shard_map/layer/pallas_call | solution.py:419
  159.0 0.0 copy-start
  159.1 1.9 %copy.18 = bf16[512,512]{1,0:T(8,128)(2,1)} copy(bf16[512,512]{1,0:T(8,128)(2,1)} %get-tuple-element.8) | data formatting | bytes 1048576
  161.0 0.0 copy-done
  161.0 0.8 copy.19
Async XLA Ops:
  0.6 0.7 copy-start.1
  0.6 1.3 copy-start.2
  159.0 1.9 %copy-start = (bf16[576,512]{1,0:T(8,128)(2,1)S(1)}, bf16[576,512]{1,0:T(8,128)(2,1)}, u32[]{:S(2)}) copy-start(bf16[576,512]{1,0:T(8,128)(2,1)} %get-tuple-element.5) | copy-start | bytes 1769476

commit v3 on v2

--- a/solution.py
+++ b/solution.py
@@ -111,7 +111,7 @@
     send, recv, pass_send, pass_recv, more_send, more_recv,
     w, dino_x, siglip_x, dino_part, siglip_part, dino_got, siglip_got, dino_gain, siglip_gain,
     block, dino_in, siglip_in, hot_d, hot_s, rest_q, rest_o, qkv_buf, ctx_buf,
-    rest_two, second, acc, keep_d, keep_s, sent_d, sent_s, back_d, back_s,
+    rest_two, second, hidden, acc, keep_d, keep_s, sent_d, sent_s, back_d, back_s,
 ):
     me, mp = lax.axis_index("dp"), lax.axis_index("mp")
     c, z, xh, y = lax.rem(me, 2), lax.rem(me // 2, 8), lax.rem(me // 16, 2), me // 32
@@ -341,61 +341,60 @@
     for r in range(8):
         rest_two[:, r * 640 : (r + 1) * 640] = dot(chosen(r), matrix(REST_TWO, QKV_D)).astype(BF)
 
-    def columns(start, j, chunk):
+    def span(start, j, chunk):
         return pl.ds(pl.multiple_of(start + j * chunk, 128), chunk)
 
-    def mlp(x, part, got, gain, at, chunk, steps, approx, keep, out, back, k):
-        extra = x.shape[1] > 1024
-
-        def rows_of(i, carry):
-            rows = pl.ds(pl.multiple_of(i * 256, 256), 256)
+    def mlp(x, part, got, gain, at, inner, chunk, approx, keep, out, back, k):
+        extra, width = x.shape[1] > 1024, x.shape[1]
+
+        def begin(i, carry):
+            rows = pl.ds(pl.multiple_of(i * 128, 128), 128)
             m = x[rows, :].astype(F32) + (part[rows, :].astype(F32) + got[rows, :].astype(F32))
             m = m.astype(BF)
             x[rows, :] = m
-            second[:, : x.shape[1]] = normed(m.astype(F32), gain[1:2, :])
+            second[rows, :width] = normed(m.astype(F32), gain[1:2, :])
+            return carry
+
+        lax.fori_loop(0, 4, begin, 0)
+
+        def lift(j, carry):
+            up = w[:, :, :, :, :, span(at, j, 256)].reshape(1024, 256)
+            raised = dot(second[:, :1024], up)
+            if extra:
+                raised = raised + dot(second[:, 1024:], rest_two[:, span(0, j, 256)])
+            hidden[:, span(0, j, 256)] = gelu(raised, approx).astype(BF)
+            return carry
+
+        lax.fori_loop(0, inner // 256, lift, 0)
+
+        def lower(which, before):
             acc[...] = jnp.zeros_like(acc)
-
-            def chunk_of(j, carry):
-                up = w[:, :, :, :, :, columns(at, j, chunk)].reshape(1024, chunk)
-                down = w[:, :, :, :, :, columns(at + steps * chunk, j, chunk)].reshape(1024, chunk)
-                raised = dot(second[:, :1024], up)
+            before()
+
+            def add(j, carry):
+                h = hidden[:, span(0, j, chunk)]
+                down = w[pl.ds(2 * which, 2), :, :, :, :, span(at + inner, j, chunk)].reshape(512, chunk)
+                acc[:, :512] += dot_t(h, down)
                 if extra:
-                    raised = raised + dot(second[:, 1024:], rest_two[:, columns(0, j, chunk)])
-                hidden = gelu(raised, approx).astype(BF)
-                acc[:, :1024] += dot_t(hidden, down)
-                if extra:
-                    acc[:, 1024:] += dot_t(hidden, rest_two[:, columns(steps * chunk, j, chunk)])
+                    more = rest_two[pl.ds(pl.multiple_of(which * 64, 64), 64), span(inner, j, chunk)]
+                    acc[:, 512:] += dot_t(h, more)
                 return carry
 
-            lax.fori_loop(0, steps, chunk_of, 0)
-
-            def put(keep_at, send_at):
-                keep[rows, :512] = x[rows, keep_at : keep_at + 512].astype(F32) + acc[:, keep_at : keep_at + 512]
-                out[rows, :512] = acc[:, send_at : send_at + 512].astype(BF)
-                if extra:
-                    ka, sa = 1024 + keep_at // 8, 1024 + send_at // 8
-                    keep[rows, 512:] = x[rows, ka : ka + 64].astype(F32) + acc[:, ka : ka + 64]
-                    out[rows, 512:] = acc[:, sa : sa + 64].astype(BF)
-
-            @pl.when(low)
-            def _():
-                put(0, 512)
-
-            @pl.when(jnp.logical_not(low))
-            def _():
-                put(512, 0)
-
-            remote(out.at[rows], back.at[rows], more_send, more_recv, k + i, "mp").start()
-            return carry
-
-        lax.fori_loop(0, 2, rows_of, 0)
-
-    mlp(siglip_x, siglip_part, siglip_got, siglip_gain, UP_S, 768, 3, True, keep_s, sent_s, back_s, 6)
-    mlp(dino_x, dino_part, dino_got, dino_gain, UP_D, 512, 4, False, keep_d, sent_d, back_d, 8)
-    for keep, out, back, k in ((keep_s, sent_s, back_s, 6), (keep_d, sent_d, back_d, 8)):
+            lax.fori_loop(0, inner // chunk, add, 0)
+
+        lower(1 - mp, lambda: None)
+        out[...] = acc[:, : out.shape[1]].astype(BF)
+        lower(mp, lambda: remote(out, back, more_send, more_recv, k, "mp").start())
+        keep[:, :512] = x[:, span(0, mp, 512)].astype(F32) + acc[:, :512]
+        if extra:
+            keep[:, 512:] = jnp.where(low, x[:, 1024:1088], x[:, 1088:]).astype(F32) + acc[:, 512:]
+
+    mlp(siglip_x, siglip_part, siglip_got, siglip_gain, UP_S, 2304, 768, True, keep_s, sent_s, back_s, 6)
+    mlp(dino_x, dino_part, dino_got, dino_gain, UP_D, 2048, 1024, False, keep_d, sent_d, back_d, 7)
+    for keep, out, back, k in ((keep_s, sent_s, back_s, 6), (keep_d, sent_d, back_d, 7)):
+        remote(out, back, more_send, more_recv, k, "mp").wait()
         for i in range(2):
             rows = slice(i * 256, (i + 1) * 256)
-            remote(out.at[rows], back.at[rows], more_send, more_recv, k + i, "mp").wait()
             result = (keep[rows, :] + back[rows, :].astype(F32)).astype(BF)
             if k == 6:
                 siglip_out[:, rows] = dot_t(hot_s[...], result).astype(BF)
@@ -422,12 +421,12 @@
         in_specs=[vmem] * 14,
         out_specs=(vmem, vmem),
         scratch_shapes=[
-            dma((n,)), dma((n,)), dma((n,)), dma((n,)), dma((10,)), dma((10,)),
+            dma((n,)), dma((n,)), dma((n,)), dma((n,)), dma((8,)), dma((8,)),
             pltpu.VMEM((Y, Z, C, XH, 8, END), BF),
             wide(1024), wide(1152), wide(1024), wide(1152), wide(1024), wide(1152), wide(1024, 2, F32), wide(1152, 2, F32),
             wide(END, 8), wide(512), pltpu.VMEM(siglip.shape, BF), wide(512, 512), wide(576, 576),
             wide(1792, 128), wide(640, 128), wide(1792, PATCHES), wide(640, PATCHES),
-            wide(5120, 128), wide(1152, 256), wide(1152, 256, F32),
+            wide(5120, 128), wide(1152), wide(2304), wide(576, rows, F32),
             wide(512, rows, F32), wide(576, rows, F32), wide(512), wide(576), wide(512), wide(576),
         ],
         compiler_params=pltpu.CompilerParams(

time: 162 us -> 166 us (1.025)
  Pallas kernels: 155 us -> 158 us
    pallas_call x1, Pallas kernels: 155 us -> 158 us  [layer(): pl.pallas_call(functools.partial(layer_kernel, streams, program), out_sha...]
where the time goes in v3:
time: 166 us; the launch traced here: 165 us
  Pallas kernels  158 us (95%)
  local copies, waits for them, and re-layouts  6.14 us (4%)
    pallas_call x1, Pallas kernels, layer(): pl.pallas_call(functools.partial(layer_kernel, streams, program), out_sha...  158 us
    unnamed x8, local copies, waits for them, and re-layouts  3.43 us

profile of v3, /device:TPU:1, one launch (start us, length us, event | category | flops | bytes accessed | tf_op | source)
XLA Modules:
  0.0 164.7 jit_solution(5540935818441586808)
XLA Ops:
  0.6 0.0 copy-start.1
  0.6 0.0 copy-start.2
  0.6 0.7 copy-done.1
  1.3 0.6 reshape.22.siglip_one
  1.9 0.0 copy-done.2
  1.9 0.6 reshape.23.siglip_two
  2.5 1.5 reshape.19.s_qkv
  4.0 157.9 %layer.1 = (bf16[512,512]{1,0:T(8,128)(2,1)}, bf16[576,512]{1,0:T(8,128)(2,1)}) custom-call(bf16[3,8,512]{2,1,0:T(8,128)(2,1)} %bitcast.13, bf16[8,512]{1,0:T(8,128)(2,1)} %bitcast.15, bf16[8,2048]{1,0:T(8,128)(2,1)} %d_up.1, bf16[8,2048]{1,0:T(8,128)(2,1)} %bitcast.12, bf16[9,1728]{1,0:T(8,128)(2,1)} %reshape.19.s_qkv, bf16[9,576]{1,0:T(8,128)(2,1)} %bitcast.14, ...), custom_call_target="tpu_custom_call" | custom-call | flops 17179869184 | bytes 33554432 | tf_op jit(solution)/shard_map/layer/pallas_call | solution.py:418
  161.9 0.0 copy-start
  161.9 1.9 %copy.18 = bf16[512,512]{1,0:T(8,128)(2,1)} copy(bf16[512,512]{1,0:T(8,128)(2,1)} %get-tuple-element.8) | data formatting | bytes 1048576
  163.9 0.0 copy-done
  163.9 0.8 copy.19
Async XLA Ops:
  0.6 0.7 copy-start.1
  0.6 1.3 copy-start.2
  161.9 1.9 %copy-start = (bf16[576,512]{1,0:T(8,128)(2,1)S(1)}, bf16[576,512]{1,0:T(8,128)(2,1)}, u32[]{:S(2)}) copy-start(bf16[576,512]{1,0:T(8,128)(2,1)} %get-tuple-element.5) | copy-start | bytes 1769476
